TPU v7x, 512 devices: a 4x2x32 block of a 4x8x32 slice. The times are simulated.
512 devices in a mesh: groups: 2 (over y), dom: 32 (over z), tilt: 4 (over x), rep: 2 (over core).
Axes of the slice: x: 4, y: 2, z: 32, core: 2. Of those that a mesh axis runs over, the one named last changes fastest.
The devices are a block of a 4x8x32 slice.
Arguments:
- patches: bfloat16 [8, 4096, 128, 128], P(('groups', 'tilt'), 'dom'), parts along dimension 0, may hold values from -6 to 6
- slot_view: int32 [8, 4096, 1], P(('groups', 'tilt'), 'dom'), parts along dimension 0, may hold values from 0 to 127, as said below
- slot_tilt: int32 [8, 4096], P(('groups', 'tilt'), 'dom'), parts along dimension 0, may hold values from 0 to 9
- slot_pos: bfloat16 [2, 8, 4096], P(None, ('groups', 'tilt'), 'dom'), parts along dimension 1, may hold values from 0 to 1
- defocus: bfloat16 [8, 4096], P(('groups', 'tilt'), 'dom'), parts along dimension 0, may hold values from 1 to 3
- projections: bfloat16 [256, 40, 2, 128, 128], P(('groups', 'dom'), 'tilt', None, 'rep'), parts along dimension 0, may hold values from -6 to 6
- warp_grid: float32 [80, 2, 256], P(('groups', 'tilt')), parts along dimension 0, may hold values from -6 to 6
Outputs:
- slot_terms: float32 [3, 8, 4096], P(None, ('groups', 'tilt'), 'dom'), parts along dimension 1
- new_warp: float32 [80, 2, 256], P(('groups', 'tilt')), parts along dimension 0
There are 2 independent parts, one for each index of `groups`. A program takes and returns all parts, laid end to end along the dimension named above; each array names one. Nothing has to cross between parts.
Inputs may be any that keep to these rules, and one draw needn't show every extreme that they name: `slot_view`: view v is owned by dom index v // 4. Among the 128 slots of one device (one tilt index and one dom index) at most 6 name views of any one owner, and in every such block some owner is named exactly 6 times.
All inputs are finite; a program needn't handle non-finite values.
Results may differ from a plain program's by a relative error of at most 0.0018.
Values may be sent and summed in bfloat16 or wider, within the bound.
No kernel may reach another device: no remote copies, remote signals or barrier semaphores. Data moves between devices by JAX's collectives and lax.ppermute only.
A program may use at most 64 MiB of HBM per device.

v0:
```python
import math

import jax
import jax.numpy as jnp
from jax import lax
from jax.sharding import PartitionSpec as P

GRID = 16


AMPLITUDE = 0.07
TRUST_FLOOR = 0.02


def copy_for_each(value, axis):
    peers = lax.axis_size(axis)
    return lax.all_to_all(
        jnp.broadcast_to(value[None], (peers, *value.shape)), axis, 0, 0, tiled=True
    )


def laid_out(tiles, dim):
    tiles = jnp.moveaxis(tiles, 0, dim)
    dims = tiles.shape
    return tiles.reshape(*dims[:dim], dims[dim] * dims[dim + 1], *dims[dim + 2 :])


def collect(value, axis, dim):
    tiles = copy_for_each(value, axis)
    return laid_out(tiles, dim)


def cut_along(value, dim, peers):
    before, after = (value.shape[:dim], value.shape[dim + 1 :])
    return jnp.moveaxis(value.reshape(*before, peers, -1, *after), dim, 0)


def sent_and_summed(value, axis, dim):
    tiles = cut_along(value, dim, lax.axis_size(axis))
    arrived = lax.all_to_all(tiles, axis, split_axis=0, concat_axis=0, tiled=True)
    return arrived.sum(axis=0)


def all_blocks(value, axes, sequence):
    tiles = value[None]
    for k in sequence:
        tiles = lax.all_gather(tiles, axes[k], axis=0, tiled=True)
    current = [lax.axis_size(axes[k]) for k in reversed(sequence)]
    tiles = tiles.reshape(*current, *value.shape)
    turned = sorted(range(len(sequence)), key=lambda place: sequence[len(sequence) - 1 - place])
    return tiles.transpose(*turned, *range(len(sequence), tiles.ndim)).reshape(-1, *value.shape)


def gathered_by_axis(value, axes, sequence, dim):
    return laid_out(all_blocks(value, axes, sequence), dim)


def signed_freq(index, pixels):
    return jnp.where(index < pixels // 2, index, index - pixels).astype(jnp.float32)


def dft_tables(freq_rows, pixels):
    columns = jnp.arange(pixels, dtype=jnp.int32)
    table_scale = 1.0 / math.sqrt(pixels)
    turns_rows = (freq_rows[:, None] * columns[None, :] % pixels).astype(jnp.float32) * (
        2.0 * math.pi / pixels
    )
    turns_full = (columns[:, None] * columns[None, :] % pixels).astype(jnp.float32) * (
        2.0 * math.pi / pixels
    )
    row_table = jnp.concatenate([jnp.cos(turns_rows), jnp.sin(turns_rows)], axis=0) * table_scale
    col_table = jnp.concatenate([jnp.cos(turns_full), jnp.sin(turns_full)], axis=1) * table_scale
    return (row_table.astype(jnp.bfloat16), col_table.astype(jnp.bfloat16))


def node_weights(pos_x, pos_y, grid_side):
    knot_pos = jnp.arange(grid_side, dtype=jnp.int32).astype(jnp.float32)
    weight_x = jnp.maximum(0.0, 1.0 - jnp.abs(pos_x[:, None] * (grid_side - 1) - knot_pos[None, :]))
    weight_y = jnp.maximum(0.0, 1.0 - jnp.abs(pos_y[:, None] * (grid_side - 1) - knot_pos[None, :]))
    return (weight_y[:, :, None] * weight_x[:, None, :]).reshape(
        pos_x.shape[0], grid_side * grid_side
    )


def spectral_terms(spectrum, ref_blk, focus_blk, shift_blk, freq_rows, pixels):
    row_total = freq_rows.shape[0]
    v_one_cos = spectrum[:, :row_total, :pixels]
    v_one_sin = spectrum[:, :row_total, pixels:]
    v_two_cos = spectrum[:, row_total:, :pixels]
    v_two_sin = spectrum[:, row_total:, pixels:]
    real_part = v_one_cos - v_two_sin
    imag_part = -(v_one_sin + v_two_cos)
    freq_y = signed_freq(freq_rows, pixels)[None, :, None]
    freq_x = signed_freq(jnp.arange(pixels, dtype=jnp.int32), pixels)[None, None, :]
    nyquist = pixels / 2.0
    radius = (freq_y * freq_y + freq_x * freq_x) / (nyquist * nyquist)
    aberration = math.pi * focus_blk[:, None, None] * radius
    contrast = -(
        math.sqrt(1.0 - AMPLITUDE * AMPLITUDE) * jnp.sin(aberration)
        + AMPLITUDE * jnp.cos(aberration)
    )
    phase_angle = (
        2.0
        * math.pi
        / pixels
        * (freq_x * shift_blk[:, 0, None, None] + freq_y * shift_blk[:, 1, None, None])
    )
    cosine = jnp.cos(phase_angle)
    sine_part = jnp.sin(phase_angle)
    ref_real = ref_blk[:, 0].astype(jnp.float32)
    ref_imag = ref_blk[:, 1].astype(jnp.float32)
    model_real = contrast * (ref_real * cosine + ref_imag * sine_part)
    model_imag = contrast * (ref_imag * cosine - ref_real * sine_part)
    diff_real = real_part - model_real
    diff_imag = imag_part - model_imag
    inverse_area = 1.0 / (pixels * pixels)
    energy = jnp.sum(diff_real * diff_real + diff_imag * diff_imag, axis=(1, 2)) * inverse_area
    cross_term = diff_imag * model_real - diff_real * model_imag
    grad_x = 2.0 * inverse_area * jnp.sum(2.0 * math.pi / pixels * freq_x * cross_term, axis=(1, 2))
    grad_y = 2.0 * inverse_area * jnp.sum(2.0 * math.pi / pixels * freq_y * cross_term, axis=(1, 2))
    return jnp.stack([energy, grad_x, grad_y], axis=1)


def on_device(patches, slot_view, slot_tilt, slot_pos, defocus, projections, warp_grid):
    owners = lax.axis_size("dom")
    rep_count = lax.axis_size("rep")
    slot_count = patches.shape[1]
    pixels = patches.shape[-1]
    view_dev = projections.shape[0]
    tilt_dev = warp_grid.shape[0]
    node_count = warp_grid.shape[2]
    capacity = 3 * slot_count // (2 * owners)
    buffer_len = owners * capacity
    chosen_view = slot_view[0, :, 0]
    owner_of = chosen_view // view_dev
    owner_hits = (owner_of[:, None] == jnp.arange(owners, dtype=jnp.int32)[None, :]).astype(
        jnp.int32
    )
    earlier = jnp.cumsum(owner_hits, axis=0) - owner_hits
    slot_rank = jnp.sum(earlier * owner_hits, axis=1)
    target = owner_of * capacity + slot_rank
    matches = target[None, :] == jnp.arange(buffer_len, dtype=jnp.int32)[:, None]
    source = jnp.sum(
        jnp.where(matches, jnp.arange(slot_count, dtype=jnp.int32)[None, :], 0), axis=1
    )
    filled = jnp.any(matches, axis=1)
    patch_rows = jnp.where(filled[:, None, None], patches[0][source], jnp.zeros((), jnp.bfloat16))
    slot_meta = jnp.stack(
        [
            slot_tilt[0].astype(jnp.float32),
            (chosen_view % view_dev).astype(jnp.float32),
            defocus[0].astype(jnp.float32),
            slot_pos[0, 0].astype(jnp.float32),
            slot_pos[1, 0].astype(jnp.float32),
            jnp.ones((slot_count,), jnp.float32),
        ],
        axis=1,
    )
    meta_rows = jnp.where(filled[:, None], slot_meta[source], 0.0).astype(jnp.bfloat16)
    patch_buffer = patch_rows.reshape(owners, capacity, pixels, pixels)
    meta_buffer = meta_rows.reshape(owners, capacity, 6)
    share_len = capacity // rep_count
    offset = lax.axis_index("rep") * share_len
    patch_send = lax.dynamic_slice_in_dim(patch_buffer, offset, share_len, 1)
    meta_send = lax.dynamic_slice_in_dim(meta_buffer, offset, share_len, 1)
    projected = collect(projections, "rep", 3)
    freq_rows = jnp.arange(pixels, dtype=jnp.int32)
    row_table, col_table = dft_tables(freq_rows, pixels)
    row_total = freq_rows.shape[0]
    projected_flat = projected.reshape(view_dev * tilt_dev, 2, row_total, pixels)
    tilt_iota = jnp.arange(tilt_dev, dtype=jnp.int32)
    view_iota = jnp.arange(view_dev, dtype=jnp.int32)

    def one_block(inputs):
        patch_blk, index_blk, focus_blk, shift_blk = inputs
        ref_blk = projected_flat[index_blk]
        first_pass = jnp.einsum(
            "fy,byx->bfx", row_table, patch_blk, preferred_element_type=jnp.float32
        ).astype(jnp.bfloat16)
        spectrum = jnp.einsum(
            "bfx,xk->bfk", first_pass, col_table, preferred_element_type=jnp.float32
        )
        return spectral_terms(spectrum, ref_blk, focus_blk, shift_blk, freq_rows, pixels)

    patch_in = lax.all_to_all(patch_send, "dom", split_axis=0, concat_axis=0, tiled=True)
    meta_in = lax.all_to_all(meta_send, "dom", split_axis=0, concat_axis=0, tiled=True)
    senders = patch_in.shape[0]
    per_sender = patch_in.shape[1]
    slot_total = senders * per_sender
    meta_flat = meta_in.reshape(slot_total, 6).astype(jnp.float32)
    tilt_match = meta_flat[:, 0:1] == tilt_iota.astype(jnp.float32)[None, :]
    view_match = meta_flat[:, 1:2] == view_iota.astype(jnp.float32)[None, :]
    tilt_local = jnp.sum(jnp.where(tilt_match, tilt_iota[None, :], 0), axis=1)
    view_local = jnp.sum(jnp.where(view_match, view_iota[None, :], 0), axis=1)
    weights = node_weights(meta_flat[:, 3], meta_flat[:, 4], GRID)
    shifts = jnp.sum(warp_grid[tilt_local] * weights[:, None, :], axis=2)
    block_len = math.gcd(slot_total, 16)
    block_count = slot_total // block_len
    per_slot = lax.map(
        one_block,
        (
            patch_in.reshape(block_count, block_len, pixels, pixels),
            (view_local * tilt_dev + tilt_local).reshape(block_count, block_len),
            meta_flat[:, 2].reshape(block_count, block_len),
            shifts.reshape(block_count, block_len, 2),
        ),
    ).reshape(slot_total, 3)
    node_coef = (
        tilt_match.astype(jnp.float32)[:, :, None]
        * per_slot[:, None, 1:3]
        * meta_flat[:, 5, None, None]
    ).reshape(senders, per_sender, 2 * tilt_dev)
    returned = lax.all_to_all(
        per_slot.reshape(senders, per_sender, 3), "dom", split_axis=0, concat_axis=0, tiled=True
    )
    weight_all = weights.reshape(senders, per_sender, node_count)
    placed = lax.dynamic_update_slice_in_dim(
        jnp.zeros((owners, capacity, 3), jnp.float32),
        returned,
        lax.axis_index("rep") * (capacity // rep_count),
        1,
    )
    own_terms = placed.reshape(buffer_len, 3)[target]
    summed = lax.psum(own_terms, "rep")
    slot_terms = summed.T[:, None, :]
    gradient = jnp.dot(
        node_coef.reshape(-1, 2 * tilt_dev).T,
        weight_all.reshape(-1, node_count),
        precision=lax.Precision.HIGHEST,
        preferred_element_type=jnp.float32,
    ).reshape(tilt_dev, 2, node_count)
    members = lax.axis_size(("dom", "rep"))
    node_share = node_count // members
    share_grad = sent_and_summed(gradient, ("dom", "rep"), 2)
    first_node = lax.axis_index(("dom", "rep")) * node_share
    warp_share = lax.dynamic_slice_in_dim(warp_grid, first_node, node_share, 2)
    moved = warp_share - share_grad / jnp.sqrt(share_grad * share_grad + TRUST_FLOOR * TRUST_FLOOR)
    new_warp = gathered_by_axis(moved, ("dom", "rep"), (0, 1), 2)
    return (slot_terms, new_warp)


def solution(mesh):
    in_specs = (
        P(("groups", "tilt"), "dom", None, None),
        P(("groups", "tilt"), "dom", None),
        P(("groups", "tilt"), "dom"),
        P(None, ("groups", "tilt"), "dom"),
        P(("groups", "tilt"), "dom"),
        P(("groups", "dom"), "tilt", None, "rep", None),
        P(("groups", "tilt"), None, None),
    )
    out_specs = (P(None, ("groups", "tilt"), "dom"), P(("groups", "tilt"), None, None))
    return jax.shard_map(
        on_device, mesh=mesh, in_specs=in_specs, out_specs=out_specs, check_vma=False
    )
```

profile of v0, /device:TPU:33, one launch (start us, length us, event | category | flops | bytes accessed | tf_op | source)
XLA Modules:
  0.0 637.8 jit_solution(5325469873337653810)
XLA Ops:
  0.6 3.7 broadcast_in_dim.130
  4.4 46.6 %all-to-all-start.2 = ((bf16[2,4,10,2,64,128]{5,4,3,2,1,0:T(8,128)(2,1)}), bf16[2,4,10,2,64,128]{5,4,3,2,1,0:T(8,128)(2,1)}, u32[]{:S(2)}, u32[]{:S(2)}) async-start(bf16[2,4,10,2,64,128]{5,4,3,2,1,0:T(8,128)(2,1)} %broadcast_in_dim.130), calls=%async_computation.2 | async-start | bytes 5242880 | tf_op jit(solution)/shard_map/all_to_all | solution.py:17
  51.1 0.2 reduce_window_sum.11
  51.3 0.2 select_reduce_fusion.1
  51.5 0.1 fusion.37
  51.6 0.1 select_reduce_fusion
  51.9 0.1 copy.127
  52.1 0.8 gather_fusion.2
  53.0 0.2 gather.26
  53.3 0.9 copy.129
  54.2 10.2 %gather_fusion.1 = bf16[192,128,128]{2,1,0:T(8,128)(2,1)} fusion(bf16[128,128,128]{2,1,0:T(8,128)(2,1)} %bitcast.208, s32[1024]{0:T(1024)S(1)} %pad_clamp_fusion.3), kind=kCustom, calls=%fused_computation.1 | custom fusion | bytes 12583680 | tf_op jit(solution)/shard_map/gather | solution.py:147
  64.5 2.1 constant_dynamic-slice_fusion.3
  66.6 2.8 copy.165
  69.4 5.5 all-to-all-start.1
  74.9 3.8 broadcast_select_fusion
  78.7 17.8 %all-to-all-done.1 = bf16[32,3,6]{2,1,0:T(4,128)(2,1)S(1)} async-done(((bf16[32,3,6]{2,1,0:T(4,128)(2,1)}), bf16[32,3,6]{2,1,0:T(4,128)(2,1)S(1)}, u32[]{:S(2)}, u32[]{:S(2)}) %all-to-all-start.1) | async-done | bytes 1184 | tf_op jit(solution)/shard_map/all_to_all | solution.py:186
  96.5 5.8 all-to-all-start
  102.4 4.0 copy.132
  106.3 0.3 fusion.45
  106.8 0.1 copy.131
  107.3 0.8 gather_fusion.3
  108.1 0.2 multiply_reduce_fusion.2
  108.8 270.8 %all-to-all-done = bf16[32,3,128,128]{2,3,1,0:T(8,128)(2,1)} async-done(((bf16[32,3,128,128]{2,3,1,0:T(8,128)(2,1)}), bf16[32,3,128,128]{2,3,1,0:T(8,128)(2,1)}, u32[]{:S(2)}, u32[]{:S(2)}) %all-to-all-start) | async-done | bytes 3145760 | tf_op jit(solution)/shard_map/all_to_all | solution.py:185
  379.5 111.2 %while.15 = (s32[]{:T(128)}, f32[6,16,3]{1,0,2:T(8,128)S(1)}, bf16[6,16,128,128]{2,3,1,0:T(8,128)(2,1)}, bf16[256,128]{1,0:T(8,128)(2,1)S(1)}, bf16[128,256]{1,0...) while((s32[]{:T(128)}, f32[6,16,3]{1,0,2:T(8,128)S(1)}, ...), condition=%wide.region_11.12_spmd.clone.clone, body=%wide.region_7.11_spmd.clone.clone.sunk | while | flops 411868064 | bytes 14461309 | solution.py:199
  379.6 4.4 fusion.63
  384.0 2.5 gather_fusion
  386.6 10.9 %add_reduce_fusion.2 = (f32[16]{0:T(128)S(1)}, f32[16,128,128]{2,1,0:T(8,128)S(1)}) fusion(f32[16,256,256]{2,1,0:T(8,128)} %fusion.63, bf16[16,2,128,128]{3,2,1,0:T(8,128)(2,1)S(1)} %gather_fusion, f32[16,128]{1,0:T(8,128)S(1)} %get-tuple-element.371, f32[16,128]{1,0:T(8,128)S(1)} %get-tuple-element.372, f32[128,128]{1,0:T(8,128)S(1)} %add_multiply_fusion.3, ...), kind=kLoop, calls=%fused_computation.31.clone.1 | loop fusion | flops 7602160 | bytes 6373504 | tf_op jit(solution)/shard_map/while/body/eval_jaxpr/reduce_sum | solution.py:117
  397.6 0.3 multiply_reduce_fusion.4
  398.1 4.4 fusion.63
  402.6 2.5 gather_fusion
  405.2 10.9 %add_reduce_fusion.2 = (f32[16]{0:T(128)S(1)}, f32[16,128,128]{2,1,0:T(8,128)S(1)}) fusion(f32[16,256,256]{2,1,0:T(8,128)} %fusion.63, bf16[16,2,128,128]{3,2,1,0:T(8,128)(2,1)S(1)} %gather_fusion, f32[16,128]{1,0:T(8,128)S(1)} %get-tuple-element.371, f32[16,128]{1,0:T(8,128)S(1)} %get-tuple-element.372, f32[128,128]{1,0:T(8,128)S(1)} %add_multiply_fusion.3, ...), kind=kLoop, calls=%fused_computation.31.clone.1 | loop fusion | flops 7602160 | bytes 6373504 | tf_op jit(solution)/shard_map/while/body/eval_jaxpr/reduce_sum | solution.py:117
  416.1 0.3 multiply_reduce_fusion.4
  416.7 4.4 fusion.63
  421.1 2.5 gather_fusion
  423.7 10.9 %add_reduce_fusion.2 = (f32[16]{0:T(128)S(1)}, f32[16,128,128]{2,1,0:T(8,128)S(1)}) fusion(f32[16,256,256]{2,1,0:T(8,128)} %fusion.63, bf16[16,2,128,128]{3,2,1,0:T(8,128)(2,1)S(1)} %gather_fusion, f32[16,128]{1,0:T(8,128)S(1)} %get-tuple-element.371, f32[16,128]{1,0:T(8,128)S(1)} %get-tuple-element.372, f32[128,128]{1,0:T(8,128)S(1)} %add_multiply_fusion.3, ...), kind=kLoop, calls=%fused_computation.31.clone.1 | loop fusion | flops 7602160 | bytes 6373504 | tf_op jit(solution)/shard_map/while/body/eval_jaxpr/reduce_sum | solution.py:117
  434.7 0.3 multiply_reduce_fusion.4
  435.2 4.4 fusion.63
  439.6 2.5 gather_fusion
  442.2 10.9 %add_reduce_fusion.2 = (f32[16]{0:T(128)S(1)}, f32[16,128,128]{2,1,0:T(8,128)S(1)}) fusion(f32[16,256,256]{2,1,0:T(8,128)} %fusion.63, bf16[16,2,128,128]{3,2,1,0:T(8,128)(2,1)S(1)} %gather_fusion, f32[16,128]{1,0:T(8,128)S(1)} %get-tuple-element.371, f32[16,128]{1,0:T(8,128)S(1)} %get-tuple-element.372, f32[128,128]{1,0:T(8,128)S(1)} %add_multiply_fusion.3, ...), kind=kLoop, calls=%fused_computation.31.clone.1 | loop fusion | flops 7602160 | bytes 6373504 | tf_op jit(solution)/shard_map/while/body/eval_jaxpr/reduce_sum | solution.py:117
  453.2 0.3 multiply_reduce_fusion.4
  453.8 4.4 fusion.63
  458.2 2.5 gather_fusion
  460.8 10.9 %add_reduce_fusion.2 = (f32[16]{0:T(128)S(1)}, f32[16,128,128]{2,1,0:T(8,128)S(1)}) fusion(f32[16,256,256]{2,1,0:T(8,128)} %fusion.63, bf16[16,2,128,128]{3,2,1,0:T(8,128)(2,1)S(1)} %gather_fusion, f32[16,128]{1,0:T(8,128)S(1)} %get-tuple-element.371, f32[16,128]{1,0:T(8,128)S(1)} %get-tuple-element.372, f32[128,128]{1,0:T(8,128)S(1)} %add_multiply_fusion.3, ...), kind=kLoop, calls=%fused_computation.31.clone.1 | loop fusion | flops 7602160 | bytes 6373504 | tf_op jit(solution)/shard_map/while/body/eval_jaxpr/reduce_sum | solution.py:117
  471.7 0.3 multiply_reduce_fusion.4
  472.3 4.4 fusion.63
  476.7 2.5 gather_fusion
  479.3 10.9 %add_reduce_fusion.2 = (f32[16]{0:T(128)S(1)}, f32[16,128,128]{2,1,0:T(8,128)S(1)}) fusion(f32[16,256,256]{2,1,0:T(8,128)} %fusion.63, bf16[16,2,128,128]{3,2,1,0:T(8,128)(2,1)S(1)} %gather_fusion, f32[16,128]{1,0:T(8,128)S(1)} %get-tuple-element.371, f32[16,128]{1,0:T(8,128)S(1)} %get-tuple-element.372, f32[128,128]{1,0:T(8,128)S(1)} %add_multiply_fusion.3, ...), kind=kLoop, calls=%fused_computation.31.clone.1 | loop fusion | flops 7602160 | bytes 6373504 | tf_op jit(solution)/shard_map/while/body/eval_jaxpr/reduce_sum | solution.py:117
  490.3 0.3 multiply_reduce_fusion.4
  491.0 0.7 copy.137
  491.6 15.0 %all-to-all-start.3 = ((f32[32,3,3]{1,2,0:T(4,128)}), f32[32,3,3]{1,2,0:T(4,128)S(1)}, u32[]{:S(2)}, u32[]{:S(2)}) async-start(f32[32,3,3]{1,2,0:T(4,128)} %copy.137), calls=%async_computation.3 | async-start | bytes 131072 | tf_op jit(solution)/shard_map/all_to_all | solution.py:213
  506.6 0.4 convolution_bitcast_fusion
  507.1 0.9 copy.144
  508.0 21.6 %all-to-all-done.3 = f32[32,3,3]{1,2,0:T(4,128)S(1)} async-done(((f32[32,3,3]{1,2,0:T(4,128)}), f32[32,3,3]{1,2,0:T(4,128)S(1)}, u32[]{:S(2)}, u32[]{:S(2)}) %all-to-all-start.3) | async-done | bytes 1184 | tf_op jit(solution)/shard_map/all_to_all | solution.py:213
  529.6 8.0 %all-to-all-start.4 = ((f32[64,10,2,4]{1,3,2,0:T(4,128)}), f32[64,10,2,4]{1,3,2,0:T(4,128)S(1)}, u32[]{:S(2)}, u32[]{:S(2)}) async-start(f32[64,10,2,4]{1,3,2,0:T(4,128)} %copy.144), calls=%async_computation.4 | async-start | bytes 524288 | tf_op jit(solution)/shard_map/all_to_all | solution.py:40
  537.8 0.7 dynamic_update_slice.11
  538.6 0.1 copy.139
  538.7 0.6 gather_fusion.4
  539.4 4.7 psum.7
  544.1 0.6 copy.149
  544.7 35.5 %all-to-all-done.4 = f32[64,10,2,4]{1,3,2,0:T(4,128)S(1)} async-done(((f32[64,10,2,4]{1,3,2,0:T(4,128)}), f32[64,10,2,4]{1,3,2,0:T(4,128)S(1)}, u32[]{:S(2)}, u32[]{:S(2)}) %all-to-all-start.4) | async-done | bytes 20512 | tf_op jit(solution)/shard_map/all_to_all | solution.py:40
  580.4 40.1 %all-gather = f32[320,2,4]{2,1,0:T(2,128)S(1)} all-gather(f32[10,2,4]{2,1,0:T(2,128)S(1)} %copy.146), channel_id=2, replica_groups=mesh['groups'=2,'dom'=32,'tilt'=4,'rep'=2] {'dom'}, dimensions={0}, use_global_device_ids=true | all-gather | bytes 10560 | tf_op jit(solution)/shard_map/all_gather | solution.py:47
  620.5 0.5 copy.147
  621.0 16.0 %all_gather.7 = f32[64,10,2,4]{1,3,2,0:T(4,128)S(1)} all-gather(f32[32,10,2,4]{1,3,2,0:T(4,128)S(1)} %copy.147), channel_id=1, replica_groups=mesh['groups'=2,'dom'=32,'tilt'=4,'rep'=2] {'rep'}, dimensions={0}, use_global_device_ids=true | all-gather | bytes 30720 | tf_op jit(solution)/shard_map/all_gather | solution.py:47
  637.1 0.7 copy.150
  (153 shorter events, 3.9 us)
Async XLA Ops:
  0.6 106.7 %copy-start = (f32[10,2,256]{2,1,0:T(2,128)S(1)}, f32[10,2,256]{2,1,0:T(2,128)}, u32[]{:S(2)}) copy-start(f32[10,2,256]{2,1,0:T(2,128)} %param.15) | copy-start | bytes 61444
  4.4 46.6 %copy-start.3 = (s32[1,128,1]{1,2,0:T(1,128)S(1)}, s32[1,128,1]{1,2,0:T(1,128)}, u32[]{:S(2)}) copy-start(s32[1,128,1]{1,2,0:T(1,128)} %param.10) | copy-start | bytes 1540
  4.4 47.5 %copy-start.1 = (bf16[2,1,128]{2,0,1:T(2,128)(2,1)S(1)}, bf16[2,1,128]{2,0,1:T(2,128)(2,1)}, u32[]{:S(2)}) copy-start(bf16[2,1,128]{2,0,1:T(2,128)(2,1)} %param.12) | copy-start | bytes 1540
  4.4 47.5 %copy-start.4 = (s32[1,128]{1,0:T(1,128)S(1)}, s32[1,128]{1,0:T(1,128)}, u32[]{:S(2)}) copy-start(s32[1,128]{1,0:T(1,128)} %param.11) | copy-start | bytes 1540
  4.4 47.5 %copy-start.2 = (bf16[1,128]{1,0:T(2,128)(2,1)S(1)}, bf16[1,128]{1,0:T(2,128)(2,1)}, u32[]{:S(2)}) copy-start(bf16[1,128]{1,0:T(2,128)(2,1)} %param.13) | copy-start | bytes 772
  4.4 65.0 %all-to-all-start.2 = ((bf16[2,4,10,2,64,128]{5,4,3,2,1,0:T(8,128)(2,1)}), bf16[2,4,10,2,64,128]{5,4,3,2,1,0:T(8,128)(2,1)}, u32[]{:S(2)}, u32[]{:S(2)}) async-start(bf16[2,4,10,2,64,128]{5,4,3,2,1,0:T(8,128)(2,1)} %broadcast_in_dim.130), calls=%async_computation.2 | async-start | bytes 5242880 | tf_op jit(solution)/shard_map/all_to_all | solution.py:17
  69.4 27.1 %all-to-all-start.1 = ((bf16[32,3,6]{2,1,0:T(4,128)(2,1)}), bf16[32,3,6]{2,1,0:T(4,128)(2,1)S(1)}, u32[]{:S(2)}, u32[]{:S(2)}) async-start(bf16[32,3,6]{2,1,0:T(4,128)(2,1)} %copy.129), calls=%async_computation.1 | async-start | bytes 65536 | tf_op jit(solution)/shard_map/all_to_all | solution.py:186
  96.5 283.0 %all-to-all-start = ((bf16[32,3,128,128]{2,3,1,0:T(8,128)(2,1)}), bf16[32,3,128,128]{2,3,1,0:T(8,128)(2,1)}, u32[]{:S(2)}, u32[]{:S(2)}) async-start(bf16[32,3,128,128]{2,3,1,0:T(8,128)(2,1)} %broadcast_select_fusion), calls=%async_computation | async-start | bytes 6291456 | tf_op jit(solution)/shard_map/all_to_all | solution.py:185
  491.6 38.0 %all-to-all-start.3 = ((f32[32,3,3]{1,2,0:T(4,128)}), f32[32,3,3]{1,2,0:T(4,128)S(1)}, u32[]{:S(2)}, u32[]{:S(2)}) async-start(f32[32,3,3]{1,2,0:T(4,128)} %copy.137), calls=%async_computation.3 | async-start | bytes 131072 | tf_op jit(solution)/shard_map/all_to_all | solution.py:213
  529.6 50.7 %all-to-all-start.4 = ((f32[64,10,2,4]{1,3,2,0:T(4,128)}), f32[64,10,2,4]{1,3,2,0:T(4,128)S(1)}, u32[]{:S(2)}, u32[]{:S(2)}) async-start(f32[64,10,2,4]{1,3,2,0:T(4,128)} %copy.144), calls=%async_computation.4 | async-start | bytes 524288 | tf_op jit(solution)/shard_map/all_to_all | solution.py:40
where the time goes:
time: 639 us; the launch traced here: 638 us
  waiting for transfers between devices  346 us (54%)
  starting transfers between devices  80.9 us (13%)
  other arithmetic  74.7 us (12%)
  blocking collectives  60.8 us (10%)
  local copies, waits for them, and re-layouts  47.4 us (7%)
  matrix products  26.8 us (4%)
    all_to_all x1, waiting for transfers between devices, on_device(): lax.all_to_all(patch_send, 'dom', split_axis=0, concat_axis=0, tiled=True)  271 us
    reduce_sum x6, other arithmetic, spectral_terms(): jnp.sum(diff_real * diff_real + diff_imag * diff_imag, axis=(1, 2))  65.7 us
    all_gather x2, blocking collectives, all_blocks(): tiles = lax.all_gather(tiles, axes[k], axis=0, tiled=True)  56.1 us
    all_to_all x1, starting transfers between devices, copy_for_each(): lax.all_to_all(jnp.broadcast_to(value[None], (peers, *value.shape)), axis...  46.6 us
    all_to_all x1, waiting for transfers between devices, sent_and_summed(): lax.all_to_all(tiles, axis, split_axis=0, concat_axis=0, tiled=True)  35.5 us
    dot_general x6, matrix products, one_block(): jnp.einsum('bfx,xk->bfk', first_pass, col_table, preferred_element_type=j...  26.4 us
    all_to_all x1, waiting for transfers between devices, on_device(): lax.all_to_all(per_slot.reshape(senders, per_sender, 3), 'dom', split_axi...  21.6 us
    all_to_all x1, waiting for transfers between devices, on_device(): lax.all_to_all(meta_send, 'dom', split_axis=0, concat_axis=0, tiled=True)  17.8 us
  transfers between devices with their start and end apart: 5, of which 4 were waited for; matrix products, arithmetic and copies ran while one was open for 5% of the time, Pallas kernels for 0%

commit v1 on v0

v1 whole, which is shorter than its diff:
```python
import functools
import math

import jax
import jax.numpy as jnp
from jax import lax
from jax.experimental import pallas as pl
from jax.experimental.pallas import tpu as pltpu
from jax.sharding import PartitionSpec as P

GRID = 16
AMPLITUDE = 0.07
TRUST_FLOOR = 0.02


def signed_freq(index, pixels):
    return jnp.where(index < pixels // 2, index, index - pixels).astype(jnp.float32)


def dft_tables(freq_rows, pixels):
    columns = jnp.arange(pixels, dtype=jnp.int32)
    table_scale = 1.0 / math.sqrt(pixels)
    turns_rows = (freq_rows[:, None] * columns[None, :] % pixels).astype(jnp.float32) * (
        2.0 * math.pi / pixels
    )
    turns_full = (columns[:, None] * columns[None, :] % pixels).astype(jnp.float32) * (
        2.0 * math.pi / pixels
    )
    row_table = jnp.concatenate([jnp.cos(turns_rows), jnp.sin(turns_rows)], axis=0) * table_scale
    col_table = jnp.concatenate([jnp.cos(turns_full), jnp.sin(turns_full)], axis=1) * table_scale
    return (row_table.astype(jnp.bfloat16), col_table.astype(jnp.bfloat16))


def node_weights(pos_x, pos_y, grid_side):
    knot_pos = jnp.arange(grid_side, dtype=jnp.int32).astype(jnp.float32)
    weight_x = jnp.maximum(0.0, 1.0 - jnp.abs(pos_x[:, None] * (grid_side - 1) - knot_pos[None, :]))
    weight_y = jnp.maximum(0.0, 1.0 - jnp.abs(pos_y[:, None] * (grid_side - 1) - knot_pos[None, :]))
    return (weight_y[:, :, None] * weight_x[:, None, :]).reshape(
        pos_x.shape[0], grid_side * grid_side
    )


def contrast_of(focus, radius):
    aberration = math.pi * focus * radius
    return -(
        math.sqrt(1.0 - AMPLITUDE * AMPLITUDE) * jnp.sin(aberration)
        + AMPLITUDE * jnp.cos(aberration)
    )


def fold_kernel(rep_ref, own_ref, recv_ref, fold_ref, spread_ref):
    first = rep_ref[0] == 0
    pairs, half, pixels = own_ref.shape[1], recv_ref.shape[3], own_ref.shape[4]
    rows = 2 * half
    col_a = lax.broadcasted_iota(jnp.int32, (pixels, pixels), 0)
    col_b = lax.broadcasted_iota(jnp.int32, (pixels, pixels), 1)
    flip_cols = ((col_a + col_b) % pixels == 0).astype(jnp.bfloat16)
    row_a = lax.broadcasted_iota(jnp.int32, (rows, 2 * rows), 0)
    row_b = lax.broadcasted_iota(jnp.int32, (rows, 2 * rows), 1)
    flip_rows = (
        (row_a // half == row_b // rows) & (row_a % half + row_b % rows == half)
    ).astype(jnp.bfloat16)
    lane = lax.broadcasted_iota(jnp.int32, (half, pixels), 1)
    line = lax.broadcasted_iota(jnp.int32, (half, pixels), 0)
    whole = jnp.logical_and(line == 0, first)
    alone = jnp.logical_or(whole, lane == pixels // 2)
    for p in range(pairs):
        near, far = [], []
        for c in range(2):
            own = own_ref[0, p, c]
            recv = recv_ref[0, p, c]
            near.append(jnp.where(first, own[:half], recv).astype(jnp.float32))
            far.append(jnp.where(first, recv, own[:half]))
            far.append(own[half:])
        mirror = jnp.dot(
            jnp.concatenate(far, axis=0), flip_cols, preferred_element_type=jnp.float32
        ).astype(jnp.bfloat16)
        mirror = jnp.dot(flip_rows, mirror, preferred_element_type=jnp.float32)
        mir_re, mir_im = mirror[:half], mirror[half:]
        even_re = jnp.where(whole, near[0], 0.5 * (near[0] + mir_re))
        even_im = jnp.where(whole, near[1], 0.5 * (near[1] - mir_im))
        odd_re = 0.5 * (near[0] - mir_re)
        odd_im = 0.5 * (near[1] + mir_im)
        base = p * rows
        fold_ref[base : base + half, :] = even_re.astype(jnp.bfloat16)
        fold_ref[base + half : base + rows, :] = even_im.astype(jnp.bfloat16)
        spread_ref[p] = jnp.where(alone, 0.0, 2.0 * (odd_re * odd_re + odd_im * odd_im))


def folded(own, recv, rep_index, total_rows):
    views, tilts, _, rows, pixels = own.shape
    half = rows // 2
    return pl.pallas_call(
        fold_kernel,
        grid=(views,),
        in_specs=[
            pl.BlockSpec(memory_space=pltpu.SMEM),
            pl.BlockSpec((1, tilts, 2, rows, pixels), lambda v: (v, 0, 0, 0, 0)),
            pl.BlockSpec((1, tilts, 2, half, pixels), lambda v: (v, 0, 0, 0, 0)),
        ],
        out_specs=[
            pl.BlockSpec((tilts * rows, pixels), lambda v: (v, 0)),
            pl.BlockSpec((tilts, half, pixels), lambda v: (v, 0, 0)),
        ],
        out_shape=[
            jax.ShapeDtypeStruct((total_rows, pixels), jnp.bfloat16),
            jax.ShapeDtypeStruct((views * tilts, half, pixels), jnp.float32),
        ],
        name="fold",
    )(rep_index, own, recv)


def on_device(patches, slot_view, slot_tilt, slot_pos, defocus, projections, warp_grid):
    owners = lax.axis_size("dom")
    rep = lax.axis_index("rep")
    slot_count = patches.shape[1]
    pixels = patches.shape[-1]
    view_dev = projections.shape[0]
    tilt_dev = warp_grid.shape[0]
    node_count = warp_grid.shape[2]
    pair_dev = view_dev * tilt_dev
    rows = projections.shape[3]
    half = rows // 2
    nyquist = pixels // 2
    capacity = 3 * slot_count // (2 * owners)
    buffer_len = owners * capacity
    first = rep == 0

    swap = [(i, 1 - i) for i in range(2)]
    recv = lax.ppermute(projections[:, :, :, half:], "rep", swap)
    main_rows = pair_dev * rows
    block_rows = -(-(3 * pair_dev) // rows) * rows
    total_rows = main_rows + block_rows
    payload, spread = folded(projections, recv, jnp.reshape(rep, (1,)).astype(jnp.int32), total_rows)
    own_col = projections[..., nyquist]
    recv_col = recv[..., nyquist]
    near_col = jnp.where(first, own_col[..., :half], recv_col)
    far_col = jnp.where(
        first,
        jnp.concatenate([recv_col, own_col[..., half:]], axis=-1)[..., 1 : half + 1],
        own_col[..., 1 : half + 1],
    )
    far_col = jnp.flip(far_col, axis=-1)
    edge_line = jnp.concatenate([projections[:, :, :, 0], near_col, far_col], axis=-1)
    payload = lax.dynamic_update_slice(payload, edge_line.reshape(3 * pair_dev, pixels), (main_rows, 0))
    gathered = lax.all_gather(payload, "dom", axis=0, tiled=True)

    chosen_view = slot_view[0, :, 0]
    tilt_local = slot_tilt[0]
    owner_of = chosen_view // view_dev
    pair_of = (chosen_view % view_dev) * tilt_dev + tilt_local
    focus = defocus[0].astype(jnp.float32)
    owner_hits = (owner_of[:, None] == jnp.arange(owners, dtype=jnp.int32)[None, :]).astype(
        jnp.int32
    )
    earlier = jnp.cumsum(owner_hits, axis=0) - owner_hits
    slot_rank = jnp.sum(earlier * owner_hits, axis=1)
    target = owner_of * capacity + slot_rank
    matches = target[None, :] == jnp.arange(buffer_len, dtype=jnp.int32)[:, None]
    asked = jnp.stack(
        [
            jnp.sum(jnp.where(matches, pair_of[None, :].astype(jnp.float32), 0.0), axis=1),
            jnp.sum(jnp.where(matches, focus[None, :], 0.0), axis=1),
        ],
        axis=1,
    ).reshape(owners, capacity * 2)

    main_y = signed_freq(rep * half + jnp.arange(half, dtype=jnp.int32), pixels)
    freq_x = signed_freq(jnp.arange(pixels, dtype=jnp.int32), pixels)
    scale_q = 1.0 / (nyquist * nyquist)
    main_q = (main_y[:, None] * main_y[:, None] + freq_x[None, :] * freq_x[None, :]) * scale_q
    heard = lax.all_to_all(asked, "dom", 0, 0, tiled=True).reshape(buffer_len, 2)
    heard_pair = heard[:, 0].astype(jnp.int32)
    heard_ctf = contrast_of(heard[:, 1, None, None], main_q[None])
    apart = jnp.sum(heard_ctf * heard_ctf * spread[heard_pair], axis=(1, 2))
    answer = lax.all_to_all(apart.reshape(owners, capacity), "dom", 0, 0, tiled=True)
    apart_slot = jnp.sum(jnp.where(matches, answer.reshape(buffer_len)[:, None], 0.0), axis=0)

    weights = node_weights(
        slot_pos[0, 0].astype(jnp.float32), slot_pos[1, 0].astype(jnp.float32), GRID
    )
    tilt_match = tilt_local[:, None] == jnp.arange(tilt_dev, dtype=jnp.int32)[None, :]
    shifts = jnp.sum(warp_grid[tilt_local] * weights[:, None, :], axis=2)
    row_table, col_table = dft_tables(
        jnp.concatenate(
            [rep * half + jnp.arange(half, dtype=jnp.int32), jnp.full((1,), nyquist, jnp.int32)]
        ),
        pixels,
    )
    main_table = jnp.concatenate([row_table[:half], row_table[half + 1 : 2 * half + 1]], axis=0)
    edge_table = jnp.concatenate([row_table[half : half + 1], row_table[2 * half + 1 :]], axis=0)

    def spectrum_of(table, count):
        first_pass = jnp.einsum(
            "fy,byx->bfx", table, patches[0], preferred_element_type=jnp.float32
        ).astype(jnp.bfloat16)
        both = jnp.einsum("bfx,xk->bfk", first_pass, col_table, preferred_element_type=jnp.float32)
        real = both[:, :count, :pixels] - both[:, count:, pixels:]
        imag = -(both[:, :count, pixels:] + both[:, count:, :pixels])
        return real, imag

    main_re, main_im = spectrum_of(main_table, half)
    edge_re, edge_im = spectrum_of(edge_table, 1)
    turn = 2.0 * math.pi / pixels
    main_phase = turn * (
        freq_x[None, None, :] * shifts[:, 0, None, None]
        + main_y[None, :, None] * shifts[:, 1, None, None]
    )
    main_cos, main_sin = jnp.cos(main_phase), jnp.sin(main_phase)
    turned_re = main_re * main_cos - main_im * main_sin
    turned_im = main_re * main_sin + main_im * main_cos
    main_ctf = contrast_of(focus[:, None, None], main_q[None])
    col_re, col_im = main_re[:, :, nyquist], main_im[:, :, nyquist]
    line_re = jnp.concatenate([edge_re[:, 0], col_re, col_re], axis=1)
    line_im = jnp.concatenate([edge_im[:, 0], col_im, -col_im], axis=1)
    line_x = jnp.concatenate([freq_x, jnp.full((2 * half,), -float(nyquist), jnp.float32)])
    line_y = jnp.concatenate([jnp.full((pixels,), -float(nyquist), jnp.float32), main_y, -main_y])
    line_weight = jnp.concatenate(
        [
            jnp.full((pixels,), jnp.where(first, 0.0, 1.0)),
            jnp.where(main_y == 0.0, 0.0, 1.0),
            jnp.where(main_y == 0.0, 0.0, 1.0),
        ]
    )
    line_q = (line_x * line_x + line_y * line_y) * scale_q
    line_phase = turn * (line_x[None] * shifts[:, 0, None] + line_y[None] * shifts[:, 1, None])
    line_cos, line_sin = jnp.cos(line_phase), jnp.sin(line_phase)
    line_ctf = contrast_of(focus[:, None], line_q[None])
    turned_line_re = line_re * line_cos - line_im * line_sin
    turned_line_im = line_re * line_sin + line_im * line_cos
    main_weight = jnp.where(
        main_y[:, None] == 0.0, 1.0, jnp.where(freq_x[None, :] == -float(nyquist), 0.0, 2.0)
    )
    held = lax.optimization_barrier(
        (
            turned_re,
            turned_im,
            main_ctf,
            turned_line_re,
            turned_line_im,
            line_ctf,
            apart_slot,
            weights,
            main_weight,
        )
    )
    (turned_re, turned_im, main_ctf, turned_line_re, turned_line_im, line_ctf) = held[:6]
    apart_slot, weights, main_weight = held[6:]

    per_owner = total_rows // rows
    ref_blk = gathered.reshape(owners * per_owner, rows, pixels)[owner_of * per_owner + pair_of]
    line_at = (owner_of * total_rows + main_rows + 3 * pair_of)[:, None] + jnp.arange(3)[None]
    line_blk = gathered[line_at.reshape(-1)].reshape(slot_count, 3 * pixels)

    def terms(spin_re, spin_im, ctf, ref_re, ref_im, weight, fx, fy, axes):
        model_re = ctf * ref_re.astype(jnp.float32)
        model_im = ctf * ref_im.astype(jnp.float32)
        diff_re = spin_re - model_re
        diff_im = spin_im - model_im
        cross = weight * (diff_im * model_re - diff_re * model_im)
        return (
            jnp.sum(weight * (diff_re * diff_re + diff_im * diff_im), axis=axes),
            jnp.sum(turn * fx * cross, axis=axes),
            jnp.sum(turn * fy * cross, axis=axes),
        )

    main_terms = terms(
        turned_re,
        turned_im,
        main_ctf,
        ref_blk[:, :half],
        ref_blk[:, half:],
        main_weight[None],
        freq_x[None, None, :],
        main_y[None, :, None],
        (1, 2),
    )
    line_len = 3 * pixels // 2
    line_terms = terms(
        turned_line_re,
        turned_line_im,
        line_ctf,
        line_blk[:, :line_len],
        line_blk[:, line_len:],
        line_weight[None],
        line_x[None],
        line_y[None],
        1,
    )
    inverse_area = 1.0 / (pixels * pixels)
    energy = (main_terms[0] + line_terms[0] + apart_slot) * inverse_area
    grad_x = 2.0 * inverse_area * (main_terms[1] + line_terms[1])
    grad_y = 2.0 * inverse_area * (main_terms[2] + line_terms[2])
    per_slot = jnp.stack([energy, grad_x, grad_y], axis=0)

    spot = tilt_match.astype(jnp.float32).T[:, None, :]
    node_coef = (spot * per_slot[None, 1:3]).reshape(2 * tilt_dev, slot_count)
    gradient = jnp.dot(
        node_coef, weights, precision=lax.Precision.HIGHEST, preferred_element_type=jnp.float32
    )
    per_slot, gradient = lax.psum((per_slot, gradient), "rep")
    slot_terms = per_slot[:, None, :]
    node_share = node_count // owners
    tiles = gradient.reshape(2 * tilt_dev, owners, node_share).transpose(1, 0, 2)
    tiles = lax.all_to_all(tiles.reshape(owners, -1), "dom", 0, 0, tiled=True)
    share_grad = jnp.sum(tiles, axis=0).reshape(tilt_dev, 2, node_share)
    warp_share = lax.dynamic_slice_in_dim(
        warp_grid, lax.axis_index("dom") * node_share, node_share, 2
    )
    moved = warp_share - share_grad / jnp.sqrt(share_grad * share_grad + TRUST_FLOOR * TRUST_FLOOR)
    spread_out = lax.all_to_all(
        jnp.broadcast_to(moved.reshape(1, -1), (owners, moved.size)), "dom", 0, 0, tiled=True
    )
    new_warp = (
        spread_out.reshape(owners, tilt_dev, 2, node_share)
        .transpose(1, 2, 0, 3)
        .reshape(tilt_dev, 2, node_count)
    )
    return (slot_terms, new_warp)


def solution(mesh):
    in_specs = (
        P(("groups", "tilt"), "dom", None, None),
        P(("groups", "tilt"), "dom", None),
        P(("groups", "tilt"), "dom"),
        P(None, ("groups", "tilt"), "dom"),
        P(("groups", "tilt"), "dom"),
        P(("groups", "dom"), "tilt", None, "rep", None),
        P(("groups", "tilt"), None, None),
    )
    out_specs = (P(None, ("groups", "tilt"), "dom"), P(("groups", "tilt"), None, None))
    return jax.shard_map(
        on_device, mesh=mesh, in_specs=in_specs, out_specs=out_specs, check_vma=False
    )
```

time: 639 us -> 415 us (0.65)
  waiting for transfers between devices: 346 us -> 192 us
  blocking collectives: 60.8 us -> 4.27 us
  other arithmetic: 74.7 us -> 51.7 us
  matrix products: 26.8 us -> 8.76 us
  between operations: 0.98 us -> 14.7 us
  starting transfers between devices: 80.9 us -> 92.9 us
    all_to_all x5 -> x4, waiting for transfers between devices: 346 us -> 62.8 us  [the longest x1 21.4 us: on_device(): tiles = lax.all_to_all(tiles.reshape(owners, -1), 'dom', 0, 0, tiled=True)]
    all_gather x0 -> x1, waiting for transfers between devices: none -> 129 us  [on_device(): gathered = lax.all_gather(payload, 'dom', axis=0, tiled=True)]
    all_gather x2 -> x0, blocking collectives: 56.1 us -> none  [all_blocks(): tiles = lax.all_gather(tiles, axes[k], axis=0, tiled=True)]
    reduce_sum x16 -> x8, other arithmetic: 68.1 us -> 18.6 us  [the longest x1 14.6 us: on_device(): apart = jnp.sum(heard_ctf * heard_ctf * spread[heard_pair], axis=(1, 2))]
    ppermute x0 -> x1, starting transfers between devices: none -> 43.4 us  [on_device(): recv = lax.ppermute(projections[:, :, :, half:], 'rep', swap)]
    all_to_all x5 -> x4, starting transfers between devices: 80.9 us -> 49.5 us  [the longest x1 21.3 us: on_device(): lax.all_to_all(apart.reshape(owners, capacity), 'dom', 0, 0, tiled=True)]
    dot_general x7 -> x5, matrix products: 26.8 us -> 8.76 us  [the longest x2 5.81 us: spectrum_of(): jnp.einsum('fy,byx->bfx', table, patches[0], preferred_element_type=jnp.f...]
    add x1 -> x4, other arithmetic: 0.01 us -> 10.8 us  [the longest x1 10.1 us: on_device(): turned_im = main_re * main_sin + main_im * main_cos]
  transfers between devices with their start and end apart: 5 -> 6, of which waited for: 4 -> 4; matrix products, arithmetic and copies ran while one was open for 5% -> 17% of each run, Pallas kernels for 0% -> 0%
where the time goes in v1:
time: 415 us; the launch traced here: 413 us
  waiting for transfers between devices  192 us (46%)
  starting transfers between devices  92.9 us (22%)
  other arithmetic  51.7 us (12%)
  local copies, waits for them, and re-layouts  44.1 us (11%)
  between operations  14.7 us (4%)
  matrix products  8.76 us (2%)
  Pallas kernels  4.42 us (1%)
  blocking collectives  4.27 us (1%)
    all_gather x1, waiting for transfers between devices, on_device(): gathered = lax.all_gather(payload, 'dom', axis=0, tiled=True)  129 us
    ppermute x1, starting transfers between devices, on_device(): recv = lax.ppermute(projections[:, :, :, half:], 'rep', swap)  43.4 us
    all_to_all x1, waiting for transfers between devices, on_device(): tiles = lax.all_to_all(tiles.reshape(owners, -1), 'dom', 0, 0, tiled=True)  21.4 us
    all_to_all x1, starting transfers between devices, on_device(): lax.all_to_all(apart.reshape(owners, capacity), 'dom', 0, 0, tiled=True)  21.3 us
    all_to_all x1, waiting for transfers between devices, on_device(): lax.all_to_all(apart.reshape(owners, capacity), 'dom', 0, 0, tiled=True)  20.9 us
    all_to_all x1, waiting for transfers between devices, on_device(): lax.all_to_all(jnp.broadcast_to(moved.reshape(1, -1), (owners, moved.size...  20.6 us
    all_to_all x1, starting transfers between devices, on_device(): tiles = lax.all_to_all(tiles.reshape(owners, -1), 'dom', 0, 0, tiled=True)  17.8 us
    reduce_sum x1, other arithmetic, on_device(): apart = jnp.sum(heard_ctf * heard_ctf * spread[heard_pair], axis=(1, 2))  14.6 us
  transfers between devices with their start and end apart: 6, of which 4 were waited for; matrix products, arithmetic and copies ran while one was open for 17% of the time, Pallas kernels for 0%

profile of v1, /device:TPU:33, one launch (start us, length us, event | category | flops | bytes accessed | tf_op | source)
XLA Modules:
  0.0 413.1 jit_solution(4934475524254021391)
XLA Ops:
  7.3 2.1 slice.122
  9.3 43.4 %collective-permute-start = (bf16[4,10,2,32,128]{4,3,2,1,0:T(8,128)(2,1)}, bf16[4,10,2,32,128]{4,3,2,1,0:T(8,128)(2,1)S(1)}, u32[]{:S(2)}, u32[]{:S(2)}) collective-permute-start(bf16[4,10,2,32,128]{4,3,2,1,0:T(8,128)(2,1)} %slice.122), channel_id=1, source_target_pairs={{0,1},{1,0},{2,3},{3,2},{4,5},{5,4},{6,7},{7,6},{8,9},{9,8},{10,11... | collective-permute-start | bytes 1966088 | tf_op jit(solution)/shard_map/ppermute | solution.py:130
  52.7 0.9 slice.124
  53.7 0.5 slice.125
  54.1 0.6 copy.107
  54.8 0.7 slice_reduce_fusion.1
  55.5 0.1 broadcast_select_fusion.1
  55.7 0.1 rev.4
  56.1 4.4 %fold.1 = (bf16[2688,128]{1,0:T(8,128)(2,1)}, f32[40,32,128]{2,1,0:T(8,128)}) custom-call(s32[1]{0:T(128)} %bitcast.21.rep_ref, bf16[4,10,2,64,128]{4,3,2,1,0:T(8,128)(2,1)} %own_ref.1, bf16[4,10,2,32,128]{4,3,2,1,0:T(8,128)(2,1)} %copy-done.7), custom_call_target="tpu_custom_call" | custom-call | tf_op jit(solution)/shard_map/fold/pallas_call | solution.py:93
  60.5 0.6 constant_dynamic-update-slice_fusion
  61.3 0.2 reduce_window_sum.11
  61.5 0.2 select_reduce_fusion.3
  61.7 0.2 select_reduce_fusion.2
  62.0 0.7 all_to_all.22
  62.7 5.7 %all-to-all-start = ((f32[32,1,12]{2,1,0:T(1,128)}), f32[32,1,12]{2,1,0:T(1,128)S(1)}, u32[]{:S(2)}, u32[]{:S(2)}) async-start(f32[32,1,12]{2,1,0:T(1,128)} %bitcast.20), calls=%async_computation | async-start | bytes 32768 | tf_op jit(solution)/shard_map/all_to_all | solution.py:172
  68.6 0.9 gather_fusion
  69.6 0.2 fusion.65
  69.8 0.2 multiply_reduce_fusion.3
  70.0 0.2 slice_reduce_fusion.3
  70.2 0.3 fusion.54
  70.7 2.9 convert_bitcast_fusion
  73.6 2.5 fusion.15
  76.1 10.1 %multiply_add_fusion = (f32[128,32,128]{2,0,1:T(8,128)}, f32[128,32,128]{2,0,1:T(8,128)S(1)}, f32[128,32,128]{2,0,1:T(8,128)S(1)}) fusion(f32[128,32]{0,1:T(8,128)S(1)} %broadcast_multiply_fusion.2, f32[128,128]{1,0:T(8,128)S(1)} %broadcast_multiply_fusion.1, f32[128,64,256]{2,0,1:T(8,128)S(1)} %fusion.15), kind=kLoop, calls=%fused_computation.34 | loop fusion | flops 4194304 | bytes 14761984 | tf_op jit(solution)/shard_map/add | solution.py:211
  86.2 1.4 copy-done
  87.6 1.2 slice_reduce_fusion
  89.0 0.2 add.383
  89.2 1.9 slice.155
  91.1 2.6 copy.105
  94.2 0.6 fusion.31
  94.7 2.9 fusion.26
  97.6 0.2 fusion.47
  97.8 0.6 multiply_add_fusion.1
  98.4 8.8 %fusion.12 = f32[128,32,128]{2,0,1:T(8,128)} fusion(f32[32,128]{1,0:T(8,128)S(1)} %add_multiply_fusion.2, f32[128]{0:T(128)S(1)} %multiply_bitcast_fusion.3), kind=kLoop, calls=%fused_computation.20 | loop fusion | flops 2621440 | bytes 2114048 | tf_op jit(solution)/shard_map/neg | solution.py:45
  107.2 9.0 %multiply_subtract_fusion = f32[128,32,128]{2,0,1:T(8,128)} fusion(f32[128,32,128]{2,0,1:T(8,128)S(1)} %copy-done.1, f32[128,32,128]{2,0,1:T(8,128)S(1)} %get-tuple-element.49, f32[128,32]{0,1:T(8,128)S(1)} %broadcast_multiply_fusion.2, f32[128,128]{1,0:T(8,128)S(1)} %broadcast_multiply_fusion.1), kind=kLoop, calls=%fused_computation.35 | loop fusion | flops 2621440 | bytes 6373376 | tf_op jit(solution)/shard_map/sub | solution.py:210
  116.3 0.5 broadcast.743
  116.8 0.7 reduce.21
  117.7 0.2 fusion.37
  117.9 2.6 gather_fusion.1
  120.5 14.6 %fusion.8 = f32[192]{0:T(256)S(1)} fusion(f32[192,32,128]{2,1,0:T(8,128)} %gather_fusion.1, f32[32,128]{1,0:T(8,128)S(1)} %add_multiply_fusion.2, f32[192]{0:T(256)S(1)} %fusion.37), kind=kLoop, calls=%fused_computation.14 | loop fusion | flops 5504832 | bytes 3163648 | tf_op jit(solution)/shard_map/reduce_sum | solution.py:175
  135.1 0.7 all_to_all.24
  135.8 21.3 %all-to-all-start.1 = ((f32[32,1,6]{2,1,0:T(1,128)}), f32[32,1,6]{2,1,0:T(1,128)S(1)}, u32[]{:S(2)}, u32[]{:S(2)}) async-start(f32[32,1,6]{2,1,0:T(1,128)} %bitcast.22), calls=%async_computation.1 | async-start | bytes 32768 | tf_op jit(solution)/shard_map/all_to_all | solution.py:176
  157.1 20.9 %all-to-all-done.1 = f32[32,1,6]{2,1,0:T(1,128)S(1)} async-done(((f32[32,1,6]{2,1,0:T(1,128)}), f32[32,1,6]{2,1,0:T(1,128)S(1)}, u32[]{:S(2)}, u32[]{:S(2)}) %all-to-all-start.1) | async-done | bytes 800 | tf_op jit(solution)/shard_map/all_to_all | solution.py:176
  177.9 0.7 reduce.22
  178.9 129.3 %all-gather.2.cloned.1.call-done = bf16[86016,128]{1,0:T(8,128)(2,1)} async-done(((bf16[2688,128]{1,0:T(8,128)(2,1)}), bf16[86016,128]{1,0:T(8,128)(2,1)}) %all-gather.2.cloned.1.call-update) | async-done | bytes 22020112 | tf_op jit(solution)/shard_map/all_gather | solution.py:146
  308.1 11.3 %gather_fusion.3 = bf16[384,128]{1,0:T(8,128)(2,1)S(1)} fusion(bf16[86016,128]{1,0:T(8,128)(2,1)} %all-gather.2.cloned.1.call-done, s32[1024]{0:T(1024)S(1)} %pad_clamp_fusion), kind=kCustom, calls=%fused_computation.3 | custom fusion | bytes 198144 | tf_op jit(solution)/shard_map/gather | solution.py:253
  319.5 8.2 %gather_fusion.2 = bf16[128,64,128]{2,1,0:T(8,128)(2,1)S(1)} fusion(bf16[1344,64,128]{2,1,0:T(8,128)(2,1)} %bitcast.119, s32[1024]{0:T(1024)S(1)} %pad_clamp_fusion.1), kind=kCustom, calls=%fused_computation.2 | custom fusion | bytes 4194816 | tf_op jit(solution)/shard_map/gather | solution.py:251
  327.7 0.4 fusion.94
  328.1 1.2 copy-done.4
  329.3 0.6 copy-done.5
  329.9 3.0 multiply_reduce_fusion.2
  332.9 0.4 multiply_reduce_fusion.1
  333.3 0.2 multiply_reduce_fusion.6
  333.7 0.3 convolution_bitcast_fusion
  334.0 0.1 copy.99
  334.1 4.3 %all-reduce.1 = (f32[3,1,128]{2,0,1:T(4,128)S(1)}, f32[32,1,160]{0,2,1:T(8,128)S(1)}) all-reduce(f32[3,1,128]{2,0,1:T(4,128)S(1)} %maximum_bitcast_fusion.2, f32[32,1,160]{0,2,1:T(8,128)S(1)} %bitcast.120), channel_id=1, replica_groups=mesh['groups'=2,'dom'=32,'tilt'=4,'rep'=2] {'rep'}, use_global_device_ids=true, to_apply=%region_13.14 | all-reduce | flops 5504 | bytes 44032 | tf_op jit(solution)/shard_map/psum | solution.py:301
  338.4 0.7 copy.100
  339.1 17.8 %all-to-all-start.2 = ((f32[32,1,160]{2,1,0:T(1,128)}), f32[32,1,160]{2,1,0:T(1,128)S(1)}, u32[]{:S(2)}, u32[]{:S(2)}) async-start(f32[32,1,160]{2,1,0:T(1,128)} %copy.100), calls=%async_computation.2 | async-start | bytes 65536 | tf_op jit(solution)/shard_map/all_to_all | solution.py:305
  356.9 21.4 %all-to-all-done.2 = f32[32,1,160]{2,1,0:T(1,128)S(1)} async-done(((f32[32,1,160]{2,1,0:T(1,128)}), f32[32,1,160]{2,1,0:T(1,128)S(1)}, u32[]{:S(2)}, u32[]{:S(2)}) %all-to-all-start.2) | async-done | bytes 20512 | tf_op jit(solution)/shard_map/all_to_all | solution.py:305
  378.6 0.6 broadcast_in_dim.154
  379.2 4.8 %all-to-all-start.3 = ((f32[32,1,160]{2,1,0:T(1,128)}), f32[32,1,160]{2,1,0:T(1,128)S(1)}, u32[]{:S(2)}, u32[]{:S(2)}) async-start(f32[32,1,160]{2,1,0:T(1,128)} %broadcast_in_dim.154), calls=%async_computation.3 | async-start | bytes 65536 | tf_op jit(solution)/shard_map/all_to_all | solution.py:311
  384.0 0.6 copy.103
  384.5 20.6 %all-to-all-done.3 = f32[32,1,160]{2,1,0:T(1,128)S(1)} async-done(((f32[32,1,160]{2,1,0:T(1,128)}), f32[32,1,160]{2,1,0:T(1,128)S(1)}, u32[]{:S(2)}, u32[]{:S(2)}) %all-to-all-start.3) | async-done | bytes 20512 | tf_op jit(solution)/shard_map/all_to_all | solution.py:311
  405.2 0.2 copy.102
  405.4 0.8 reshape.722
  (93 shorter events, 3.0 us)
Async XLA Ops:
  7.2 46.5 %copy-start.3 = (bf16[4,10,2,64,128]{4,3,2,1,0:T(8,128)(2,1)S(1)}, bf16[4,10,2,64,128]{4,3,2,1,0:T(8,128)(2,1)}, u32[]{:S(2)}) copy-start(bf16[4,10,2,64,128]{4,3,2,1,0:T(8,128)(2,1)} %own_ref.1) | copy-start | bytes 3932164
  7.2 300.9 %all-gather.2.cloned.1.call-start = ((), (), s32[]{:S(2)}) async-start(), calls=%async_computation.4 | async-start | bytes 22708224 | tf_op jit(solution)/shard_map/all_gather | solution.py:146
  9.3 45.5 %collective-permute-start = (bf16[4,10,2,32,128]{4,3,2,1,0:T(8,128)(2,1)}, bf16[4,10,2,32,128]{4,3,2,1,0:T(8,128)(2,1)S(1)}, u32[]{:S(2)}, u32[]{:S(2)}) collective-permute-start(bf16[4,10,2,32,128]{4,3,2,1,0:T(8,128)(2,1)} %slice.122), channel_id=1, source_target_pairs={{0,1},{1,0},{2,3},{3,2},{4,5},{5,4},{6,7},{7,6},{8,9},{9,8},{10,11... | collective-permute-start | bytes 1966088 | tf_op jit(solution)/shard_map/ppermute | solution.py:130
  54.7 6.5 %copy-start.8 = (s32[1,128]{1,0:T(1,128)S(1)}, s32[1,128]{1,0:T(1,128)}, u32[]{:S(2)}) copy-start(s32[1,128]{1,0:T(1,128)} %param.9) | copy-start | bytes 1540
  54.7 6.5 %copy-start.10 = (s32[1,128,1]{1,2,0:T(1,128)S(1)}, s32[1,128,1]{1,2,0:T(1,128)}, u32[]{:S(2)}) copy-start(s32[1,128,1]{1,2,0:T(1,128)} %param.8) | copy-start | bytes 1540
  54.7 6.9 %copy-start.11 = (bf16[1,128]{1,0:T(2,128)(2,1)S(1)}, bf16[1,128]{1,0:T(2,128)(2,1)}, u32[]{:S(2)}) copy-start(bf16[1,128]{1,0:T(2,128)(2,1)} %param.11) | copy-start | bytes 772
  54.8 13.6 %copy-start.9 = (bf16[2,1,128]{2,0,1:T(2,128)(2,1)S(1)}, bf16[2,1,128]{2,0,1:T(2,128)(2,1)}, u32[]{:S(2)}) copy-start(bf16[2,1,128]{2,0,1:T(2,128)(2,1)} %param.10) | copy-start | bytes 1540
  54.8 1.2 copy-start.7
  55.5 13.1 %copy-start.6 = (f32[10,2,256]{2,1,0:T(2,128)S(1)}, f32[10,2,256]{2,1,0:T(2,128)}, u32[]{:S(2)}) copy-start(f32[10,2,256]{2,1,0:T(2,128)} %param.13) | copy-start | bytes 61444
  62.7 53.6 %all-to-all-start = ((f32[32,1,12]{2,1,0:T(1,128)}), f32[32,1,12]{2,1,0:T(1,128)S(1)}, u32[]{:S(2)}, u32[]{:S(2)}) async-start(f32[32,1,12]{2,1,0:T(1,128)} %bitcast.20), calls=%async_computation | async-start | bytes 32768 | tf_op jit(solution)/shard_map/all_to_all | solution.py:172
  86.2 1.4 copy-start
  97.6 9.6 %copy-start.1 = (f32[128,32,128]{2,0,1:T(8,128)S(1)}, f32[128,32,128]{2,0,1:T(8,128)}, u32[]{:S(2)}) copy-start(f32[128,32,128]{2,0,1:T(8,128)} %copy-done) | copy-start | bytes 6291460
  107.2 10.7 %copy-start.2 = (f32[40,32,128]{2,1,0:T(8,128)S(1)}, f32[40,32,128]{2,1,0:T(8,128)}, u32[]{:S(2)}) copy-start(f32[40,32,128]{2,1,0:T(8,128)} %get-tuple-element.13) | copy-start | bytes 1966084
  135.8 42.1 %all-to-all-start.1 = ((f32[32,1,6]{2,1,0:T(1,128)}), f32[32,1,6]{2,1,0:T(1,128)S(1)}, u32[]{:S(2)}, u32[]{:S(2)}) async-start(f32[32,1,6]{2,1,0:T(1,128)} %bitcast.22), calls=%async_computation.1 | async-start | bytes 32768 | tf_op jit(solution)/shard_map/all_to_all | solution.py:176
  327.7 1.6 copy-start.4
  327.7 2.2 copy-start.5
  339.1 39.2 %all-to-all-start.2 = ((f32[32,1,160]{2,1,0:T(1,128)}), f32[32,1,160]{2,1,0:T(1,128)S(1)}, u32[]{:S(2)}, u32[]{:S(2)}) async-start(f32[32,1,160]{2,1,0:T(1,128)} %copy.100), calls=%async_computation.2 | async-start | bytes 65536 | tf_op jit(solution)/shard_map/all_to_all | solution.py:305
  379.2 25.9 %all-to-all-start.3 = ((f32[32,1,160]{2,1,0:T(1,128)}), f32[32,1,160]{2,1,0:T(1,128)S(1)}, u32[]{:S(2)}, u32[]{:S(2)}) async-start(f32[32,1,160]{2,1,0:T(1,128)} %broadcast_in_dim.154), calls=%async_computation.3 | async-start | bytes 65536 | tf_op jit(solution)/shard_map/all_to_all | solution.py:311
Sparse Core Ops, SparseCore 0:
  61.3 246.8 all-gather.1

commit v2 on v0

v2 whole, which is shorter than its diff:
```python
import functools
import math

import jax
import jax.numpy as jnp
import numpy as np
from jax import lax
from jax.experimental import pallas as pl
from jax.experimental.pallas import tpu as pltpu
from jax.sharding import PartitionSpec as P


GRID = 16
AMPLITUDE = 0.07
TRUST_FLOOR = 0.02
RADIUS = 8
CHUNKS = 2
GROUP = 8
EXTRA = 4
BIG = math.sqrt(1.0 - AMPLITUDE * AMPLITUDE)


def signed_freq(pixels):
    index = np.arange(pixels)
    return np.where(index < pixels // 2, index, index - pixels).astype(np.float32)


def dft_tables(pixels):
    index = np.arange(pixels)
    angle = (index[:, None] * index[None, :] % pixels) * (2.0 * math.pi / pixels)
    scale = 1.0 / math.sqrt(pixels)
    return tuple(
        np.asarray(t * scale, np.float32).astype(jnp.bfloat16) for t in (np.cos(angle), np.sin(angle))
    )


def node_weights(pos_x, pos_y, grid_side):
    knot_pos = jnp.arange(grid_side, dtype=jnp.int32).astype(jnp.float32)
    weight_x = jnp.maximum(0.0, 1.0 - jnp.abs(pos_x[:, None] * (grid_side - 1) - knot_pos[None, :]))
    weight_y = jnp.maximum(0.0, 1.0 - jnp.abs(pos_y[:, None] * (grid_side - 1) - knot_pos[None, :]))
    return (weight_y[:, :, None] * weight_x[:, None, :]).reshape(
        pos_x.shape[0], grid_side * grid_side
    )


def iota(shape, dim):
    return lax.broadcasted_iota(jnp.int32, shape, dim)


def line_dot(a, b):
    return lax.dot_general(a, b, (((1,), (1,)), ((), ())), preferred_element_type=jnp.float32)


def fold_kernel(rep_ref, own_ref, recv_ref, out_ref, spread_ref):
    first = rep_ref[0] == 0
    views, tilts, half, pixels = own_ref.shape[0], own_ref.shape[1], own_ref.shape[3], own_ref.shape[4]
    flip_cols = ((iota((pixels, pixels), 0) + iota((pixels, pixels), 1)) % pixels == 0).astype(
        jnp.bfloat16
    )
    row_a, row_b = iota((2 * half, 2 * half), 0), iota((2 * half, 2 * half), 1)
    flip_rows = (
        (row_a // half == row_b // half) & (row_a % half + row_b % half == half)
    ).astype(jnp.bfloat16)
    at_edge = (iota((16, pixels), 1) == pixels // 2).astype(jnp.bfloat16)
    lane, line = iota((half, pixels), 1), iota((half, pixels), 0)
    whole = line == 0
    alone = jnp.logical_or(whole, lane == pixels // 2)
    count = views * tilts
    extras = []
    batch = 5
    for start in range(0, count, batch):
        lows, boths = [], []
        for p in range(start, start + batch):
            v, t = p // tilts, p % tilts
            own, recv = own_ref[v, t], recv_ref[v, t]
            lows.append(jnp.where(first, own, recv).reshape(2 * half, pixels))
            boths.append(jnp.where(first, recv, own).reshape(2 * half, pixels))
        turned = jnp.dot(
            jnp.concatenate(boths, axis=0), flip_cols, preferred_element_type=jnp.float32
        ).astype(jnp.bfloat16)
        mirrors = [
            jnp.dot(
                flip_rows,
                turned[2 * half * i : 2 * half * (i + 1)],
                preferred_element_type=jnp.float32,
            )
            for i in range(batch)
        ]
        cols = [
            line_dot(at_edge, jnp.concatenate([low, mirror.astype(jnp.bfloat16)], axis=0))
            for low, mirror in zip(lows, mirrors, strict=True)
        ]
        for i in range(batch):
            p = start + i
            low, mirror = lows[i].astype(jnp.float32), mirrors[i]
            low_re, low_im, mir_re, mir_im = low[:half], low[half:], mirror[:half], mirror[half:]
            base = p * 2 * half
            even_re = jnp.where(whole, low_re, 0.5 * (low_re + mir_re))
            even_im = jnp.where(whole, low_im, 0.5 * (low_im - mir_im))
            out_ref[base : base + half, :] = even_re.astype(jnp.bfloat16)
            out_ref[base + half : base + 2 * half, :] = even_im.astype(jnp.bfloat16)
            odd_re, odd_im = 0.5 * (low_re - mir_re), 0.5 * (low_im + mir_im)
            spread_ref[p] = jnp.where(alone, 0.0, 2.0 * (odd_re * odd_re + odd_im * odd_im))
            both = boths[i].astype(jnp.float32)
            col = cols[i][0:1]
            extras += [
                both[0:1],
                both[half : half + 1],
                jnp.concatenate([col[:, :half], col[:, 2 * half : 3 * half]], axis=1),
                jnp.concatenate([col[:, half : 2 * half], col[:, 3 * half :]], axis=1),
            ]
    top = count * 2 * half
    for g in range(count * EXTRA // 16):
        out_ref[top + 16 * g : top + 16 * (g + 1), :] = jnp.concatenate(
            extras[16 * g : 16 * (g + 1)], axis=0
        ).astype(jnp.bfloat16)


def folded(own, recv, rep_index, chunk):
    views, tilts, _, half, pixels = own.shape
    per = views // CHUNKS
    count = per * tilts
    rows = count * (2 * half + EXTRA)
    return pl.pallas_call(
        fold_kernel,
        grid=(1,),
        in_specs=[
            pl.BlockSpec(memory_space=pltpu.SMEM),
            pl.BlockSpec((per, tilts, 2, half, pixels), lambda v: (chunk, 0, 0, 0, 0)),
            pl.BlockSpec((per, tilts, 2, half, pixels), lambda v: (chunk, 0, 0, 0, 0)),
        ],
        out_specs=[
            pl.BlockSpec((rows, pixels), lambda v: (0, 0)),
            pl.BlockSpec((count, half, pixels), lambda v: (0, 0, 0)),
        ],
        out_shape=[
            jax.ShapeDtypeStruct((rows, pixels), jnp.bfloat16),
            jax.ShapeDtypeStruct((count, half, pixels), jnp.float32),
        ],
        name="fold",
    )(rep_index, own, recv)


def dft_kernel(src_ref, patch_ref, row_ref, col_ref, side_ref, rt_ref, ct_ref, *outs, start):
    out_re, out_im, out_ctf, edge_ref = outs
    step = pl.program_id(0) + start
    pixels = col_ref.shape[0]
    half = pixels // 2
    rt = rt_ref[0]
    for k in range(GROUP):
        patch = patch_ref[src_ref[step * GROUP + k]]
        first = jnp.dot(row_ref[...], patch, preferred_element_type=jnp.float32).astype(jnp.bfloat16)
        both = jnp.dot(first, col_ref[...], preferred_element_type=jnp.float32)
        re = both[:half, :pixels] - both[half:pixels, pixels:]
        im = -(both[:half, pixels:] + both[half:pixels, :pixels])
        cy, sy = rt[:, k : k + 1], rt[:, GROUP + k : GROUP + k + 1]
        qc = rt[:, 2 * GROUP + k : 2 * GROUP + k + 1]
        qs = rt[:, 3 * GROUP + k : 3 * GROUP + k + 1]
        cx, sx, pc, ps = (ct_ref[i, k : k + 1, :] for i in range(4))
        er = cy * cx - sy * sx
        ei = sy * cx + cy * sx
        out_re[k] = re * er - im * ei
        out_im[k] = re * ei + im * er
        out_ctf[k] = qc * pc + qs * ps
        side = line_dot(side_ref[...], first[:pixels])
        low, high = both[pixels : pixels + 1], both[pixels + 1 : pixels + 2]
        edge_ref[0, k : k + 1, :] = low[:, :pixels] - high[:, pixels:]
        edge_ref[1, k : k + 1, :] = -(low[:, pixels:] + high[:, :pixels])
        edge_ref[2, k : k + 1, :] = side[0:1]
        edge_ref[3, k : k + 1, :] = side[1:2]


def spectra(src, patches, row_table, col_table, side_table, row_tab, col_tab, start, groups):
    _, half, pixels = row_tab.shape
    slots = groups * GROUP
    tall = row_table.shape[0]
    plane = pl.BlockSpec((GROUP, half, pixels), lambda g: (g, 0, 0))
    shape = jax.ShapeDtypeStruct((slots, half, pixels), jnp.float32)
    return pl.pallas_call(
        functools.partial(dft_kernel, start=start),
        grid=(groups,),
        in_specs=[
            pl.BlockSpec(memory_space=pltpu.SMEM),
            pl.BlockSpec(patches.shape, lambda g: (0, 0, 0)),
            pl.BlockSpec((tall, pixels), lambda g: (0, 0)),
            pl.BlockSpec((pixels, 2 * pixels), lambda g: (0, 0)),
            pl.BlockSpec(side_table.shape, lambda g: (0, 0)),
            pl.BlockSpec((1, half, pixels), lambda g: (g + start, 0, 0)),
            pl.BlockSpec((4, GROUP, pixels), lambda g: (0, g + start, 0)),
        ],
        out_specs=[plane, plane, plane, pl.BlockSpec((4, GROUP, pixels), lambda g: (0, g, 0))],
        out_shape=[shape, shape, shape, jax.ShapeDtypeStruct((4, slots, pixels), jnp.float32)],
        cost_estimate=pl.CostEstimate(flops=10**9 * groups, bytes_accessed=2 * 10**7, transcendentals=0),
        name="spectra",
    )(src, patches, row_table, col_table, side_table, row_tab, col_tab)


def chosen(refs, pair, start, size, stride):
    per = refs[0][1]
    rows = None
    for i, (ref, count) in enumerate(refs):
        q = jnp.clip(pair - i * per, 0, count - 1)
        at = pl.multiple_of(start(count, q), stride)
        part = ref[pl.ds(at, size), :]
        rows = part if rows is None else jnp.where(pair >= i * per, part, rows)
    return rows


def extra_rows(refs, pair, pixels):
    return chosen(refs, pair, lambda n, q: n * pixels + (q // 4) * 16, 16, 16)


def terms_kernel(ids_ref, *refs, sources, base, cap):
    at, held_by = 0, []
    for counts, _ in sources:
        held_by.append(list(zip(refs[at : at + len(counts)], counts, strict=True)))
        at += len(counts)
    re_ref, im_ref, ctf_ref, line_ref, out_ref = refs[at:]
    _, half, pixels = re_ref.shape
    line, lane = iota((half, pixels), 0), iota((half, pixels), 1)
    weight = jnp.where(line == 0, 1.0, jnp.where(lane == half, 0.0, 2.0))
    fy = line.astype(jnp.float32)
    edge = iota((1, pixels), 1)
    col_weight = jnp.where(edge % half == 0, 0.0, 1.0)
    col_fy = jnp.where(edge < half, edge, half - edge).astype(jnp.float32)
    for n, (counts, fixed) in enumerate(sources):
        held = held_by[n]
        for k in range(cap):
            i = n * cap + k
            pair = jnp.int32(k) if fixed else ids_ref[base + i]
            ref_blk = chosen(held, pair, lambda m, q: q * pixels, pixels, pixels).astype(jnp.float32)
            group = extra_rows(held, pair, pixels)
            picker = iota((8, 16), 1) == 4 * ((pair % counts[0]) % 4) + iota((8, 16), 0)
            rim = jnp.dot(picker.astype(jnp.bfloat16), group, preferred_element_type=jnp.float32)
            ctf = ctf_ref[i]
            mod_re, mod_im = ctf * ref_blk[:half], ctf * ref_blk[half:]
            dif_re, dif_im = re_ref[i] - mod_re, im_ref[i] - mod_im
            power = weight * (dif_re * dif_re + dif_im * dif_im)
            cross = weight * (dif_im * mod_re - dif_re * mod_im)
            own = [line_ref[j, i : i + 1, :] for j in range(6)]

            def edge_terms(a, b, own=own, rim=rim):
                m_re, m_im = own[a + 2] * rim[b : b + 1], own[a + 2] * rim[b + 1 : b + 2]
                d_re, d_im = own[a] - m_re, own[a + 1] - m_im
                return d_re * d_re + d_im * d_im, d_im * m_re - d_re * m_im

            row_power, row_cross = edge_terms(0, 0)
            col_power, col_cross = edge_terms(3, 2)
            col_cross = col_weight * col_cross
            out_ref[0, i : i + 1, :] = (
                jnp.sum(power, axis=0, keepdims=True) + row_power + col_weight * col_power
            )
            out_ref[1, i : i + 1, :] = jnp.sum(cross, axis=0, keepdims=True) + row_cross
            out_ref[2, i : i + 1, :] = (
                jnp.sum(fy * cross, axis=0, keepdims=True) - half * row_cross + col_fy * col_cross
            )
            out_ref[3, i : i + 1, :] = col_cross


def terms_of(first_hop, ids, sources, turned, cap):
    re, im, ctf, line = turned
    _, half, pixels = re.shape
    number = len(sources) * cap
    arrays = [a for blocks, _, _ in sources for a in blocks]
    plane = pl.BlockSpec((number, half, pixels), lambda g: (0, 0, 0))
    return pl.pallas_call(
        functools.partial(
            terms_kernel, sources=[(c, f) for _, c, f in sources], base=first_hop * cap, cap=cap
        ),
        grid=(1,),
        in_specs=[pl.BlockSpec(memory_space=pltpu.SMEM)]
        + [pl.BlockSpec(a.shape, lambda g: (0, 0)) for a in arrays]
        + [plane, plane, plane, pl.BlockSpec(line.shape, lambda g: (0, 0, 0))],
        out_specs=pl.BlockSpec((4, number, pixels), lambda g: (0, 0, 0)),
        out_shape=jax.ShapeDtypeStruct((4, number, pixels), jnp.float32),
        cost_estimate=pl.CostEstimate(flops=10**9, bytes_accessed=10**7, transcendentals=0),
        name="terms",
    )(ids, *arrays, re, im, ctf, line)


def pick_kernel(ids_ref, *refs, counts, cap, caps):
    held = list(zip(refs[: len(counts)], counts, strict=True))
    pixels = refs[0].shape[1]
    for j, out in enumerate(refs[len(counts) :]):
        groups = [None] * (-(-caps[j] * EXTRA // 16))
        for k in range(caps[j]):
            pair = ids_ref[j * cap + k]
            out[k * pixels : (k + 1) * pixels, :] = chosen(
                held, pair, lambda n, q: q * pixels, pixels, pixels
            )
            group = extra_rows(held, pair, pixels)
            row, col = iota((16, 16), 0), iota((16, 16), 1)
            mover = (row // 4 == k % 4) & (col // 4 == (pair % counts[0]) % 4) & (row % 4 == col % 4)
            moved = jnp.dot(mover.astype(jnp.bfloat16), group, preferred_element_type=jnp.float32)
            g = k // 4
            groups[g] = moved if groups[g] is None else groups[g] + moved
        for g, rows in enumerate(groups):
            at = caps[j] * pixels + 16 * g
            out[at : at + 16, :] = rows.astype(jnp.bfloat16)


def picked(ids, blocks, counts, cap, caps):
    pixels = blocks[0].shape[1]
    rows = [c * pixels + 16 * (-(-c * EXTRA // 16)) for c in caps]
    return pl.pallas_call(
        functools.partial(pick_kernel, counts=counts, cap=cap, caps=caps),
        grid=(1,),
        in_specs=[pl.BlockSpec(memory_space=pltpu.SMEM)]
        + [pl.BlockSpec(b.shape, lambda g: (0, 0)) for b in blocks],
        out_specs=[pl.BlockSpec((r, pixels), lambda g: (0, 0)) for r in rows],
        out_shape=[jax.ShapeDtypeStruct((r, pixels), jnp.bfloat16) for r in rows],
        name="pick",
    )(ids, *blocks)


def apart_kernel(ids_ref, *refs, counts):
    held = refs[: len(counts)]
    rt_ref, ct_ref, out_ref = refs[len(counts) :]
    step = pl.program_id(0)
    rt = rt_ref[0]
    for k in range(GROUP):
        pair = ids_ref[step * GROUP + k]
        power = None
        for i, (ref, count) in enumerate(zip(held, counts, strict=True)):
            part = ref[jnp.clip(pair - i * counts[0], 0, count - 1)]
            power = part if power is None else jnp.where(pair >= i * counts[0], part, power)
        ctf = (
            rt[:, k : k + 1] * ct_ref[0, k : k + 1, :]
            + rt[:, GROUP + k : GROUP + k + 1] * ct_ref[1, k : k + 1, :]
        )
        out_ref[k : k + 1, :] = jnp.sum(ctf * ctf * power, axis=0, keepdims=True)


def apart_of(ids, spreads, counts, row_tab, col_tab):
    groups, half, pixels = row_tab.shape
    return pl.pallas_call(
        functools.partial(apart_kernel, counts=counts),
        grid=(groups,),
        in_specs=[pl.BlockSpec(memory_space=pltpu.SMEM)]
        + [pl.BlockSpec(s.shape, lambda g: (0, 0, 0)) for s in spreads]
        + [
            pl.BlockSpec((1, half, pixels), lambda g: (g, 0, 0)),
            pl.BlockSpec((2, GROUP, pixels), lambda g: (0, g, 0)),
        ],
        out_specs=pl.BlockSpec((GROUP, pixels), lambda g: (g, 0)),
        out_shape=jax.ShapeDtypeStruct((groups * GROUP, pixels), jnp.float32),
        cost_estimate=pl.CostEstimate(flops=10**9, bytes_accessed=4 * 10**6, transcendentals=0),
        name="apart",
    )(ids, *spreads, row_tab, col_tab)


def lane_tables(tables, pixels):
    stacked = jnp.stack(tables, axis=0)
    count, slots, rows = stacked.shape
    laid = stacked.reshape(count, slots // GROUP, GROUP, rows).transpose(1, 3, 0, 2)
    laid = laid.reshape(slots // GROUP, rows, count * GROUP)
    return jnp.pad(laid, ((0, 0), (0, 0), (0, pixels - count * GROUP)))


def contrast_tables(focus, low_y, freq_x, nyquist):
    rate = math.pi * focus[:, None] / (nyquist * nyquist)
    by, bx = rate * (low_y * low_y)[None], rate * (freq_x * freq_x)[None]
    sin_x, cos_x = jnp.sin(bx), jnp.cos(bx)
    pc = -(BIG * sin_x + AMPLITUDE * cos_x)
    ps = -(BIG * cos_x - AMPLITUDE * sin_x)
    return jnp.cos(by), jnp.sin(by), pc, ps


def contrast_of(focus, radius):
    aberration = math.pi * focus * radius
    return -(BIG * jnp.sin(aberration) + AMPLITUDE * jnp.cos(aberration))


def on_device(patches, slot_view, slot_tilt, slot_pos, defocus, projections, warp_grid):
    owners = lax.axis_size("dom")
    me = lax.axis_index("dom")
    rep = lax.axis_index("rep")
    first = rep == 0
    slot_count = patches.shape[1]
    pixels = patches.shape[-1]
    half = nyquist = pixels // 2
    view_dev = projections.shape[0]
    tilt_dev = warp_grid.shape[0]
    node_count = warp_grid.shape[2]
    pair_dev = view_dev * tilt_dev
    cap = 3 * slot_count // (2 * owners)
    reach = owners // 2
    hops = reach + 1
    used = hops * cap
    slots = -(-used // GROUP) * GROUP
    counts = (pair_dev // CHUNKS,) * CHUNKS
    turn = 2.0 * math.pi / pixels
    scale_q = 1.0 / (nyquist * nyquist)

    recv = lax.ppermute(projections, "rep", [(0, 1), (1, 0)])
    rep_index = jnp.reshape(rep, (1,)).astype(jnp.int32)
    made = []
    for c in range(CHUNKS):
        made.append(folded(projections, recv, rep_index, c))
    blocks = [m[0] for m in made]
    spreads = [m[1] for m in made]

    def ring(shift):
        pairs = []
        for i in range(owners):
            pairs.append((2 * i, 2 * ((i + shift) % owners)))
            pairs.append((2 * i + 1, 2 * ((i - shift) % owners) + 1))
        return pairs

    ring_blocks = [blocks]
    for _ in range(1, RADIUS + 1):
        sent = []
        for block in ring_blocks[-1]:
            sent.append(lax.ppermute(block, ("dom", "rep"), ring(1)))
        ring_blocks.append(sent)

    later = made[0][1][0, 0, 0].astype(jnp.int32)

    chosen_view = slot_view[0, :, 0]
    owner_of = chosen_view // view_dev
    pair_of = (chosen_view % view_dev) * tilt_dev + slot_tilt[0]
    hits = (owner_of[:, None] == jnp.arange(owners, dtype=jnp.int32)[None, :]).astype(jnp.int32)
    earlier = jnp.cumsum(hits, axis=0) - hits
    rank = jnp.sum(earlier * hits, axis=1)
    behind = (me - owner_of) % owners
    is_behind = (behind >= 1) & (behind <= reach)
    hop_of = jnp.where(is_behind, behind, (owners - behind) % owners)
    side_of = jnp.where(is_behind, 0, 1)
    share = cap // 2
    opposite = behind == reach
    side_of = jnp.where(opposite, jnp.where(rank < cap - share, 0, 1), side_of)
    rank = jnp.where(opposite & (side_of == 1), rank - (cap - share), rank)
    lane_of = hop_of * cap + rank
    place = (lane_of[None, :] == jnp.arange(slots, dtype=jnp.int32)[:, None]) & (
        side_of[None, :] == rep
    )

    def listed(values):
        return jnp.sum(jnp.where(place, values[None, :], jnp.zeros((), values.dtype)), axis=1)

    src = listed(jnp.arange(slot_count, dtype=jnp.int32))
    pair_at = listed(pair_of)
    tilt_at = listed(slot_tilt[0])
    focus = listed(defocus[0].astype(jnp.float32))
    pos_x = listed(slot_pos[0, 0].astype(jnp.float32))
    pos_y = listed(slot_pos[1, 0].astype(jnp.float32))
    valid = jnp.any(place, axis=1).astype(jnp.float32)

    peers = jnp.arange(owners, dtype=jnp.int32)
    hop_iota = jnp.arange(hops, dtype=jnp.int32)
    away = jnp.where(first, me - peers, peers - me) % owners
    pair_list = pair_at[:used].reshape(hops, cap).astype(jnp.float32)
    focus_list = focus[:used].reshape(hops, cap)
    near_hit = away[:, None] == hop_iota[None, :]
    far_hit = (away[:, None] + RADIUS == hop_iota[None, :]) & (away[:, None] >= 1)

    def rows_of(hit, table):
        return jnp.sum(jnp.where(hit[:, :, None], table[None], 0.0), axis=1)

    asked = jnp.concatenate(
        [rows_of(near_hit, pair_list), rows_of(near_hit, focus_list), rows_of(far_hit, pair_list)],
        axis=1,
    )
    heard = lax.all_to_all(asked, "dom", 0, 0, tiled=True)

    low_y = np.arange(half).astype(np.float32)
    freq_x = signed_freq(pixels)

    focus, pos_x, pos_y, tilt_at, src = (
        v + later.astype(v.dtype) for v in (focus, pos_x, pos_y, tilt_at, src)
    )
    weights = node_weights(pos_x, pos_y, GRID)
    tilt_match = tilt_at[:, None] == jnp.arange(tilt_dev, dtype=jnp.int32)[None, :]
    all_shift = jnp.dot(
        weights,
        warp_grid.reshape(tilt_dev * 2, node_count).T,
        precision=lax.Precision.HIGHEST,
        preferred_element_type=jnp.float32,
    ).reshape(slots, tilt_dev, 2)
    shifts = jnp.sum(jnp.where(tilt_match[:, :, None], all_shift, 0.0), axis=1)
    shift_x, shift_y = shifts[:, 0:1], shifts[:, 1:2]
    cos_table, sin_table = dft_tables(pixels)
    zeros = np.zeros((14, pixels), jnp.bfloat16)
    edge_rows = [cos_table[half : half + 1], sin_table[half : half + 1], zeros]
    row_table = jnp.asarray(np.concatenate([cos_table[:half], sin_table[:half]] + edge_rows, axis=0))
    side_table = jnp.asarray(np.concatenate(edge_rows, axis=0))
    col_table = jnp.asarray(np.concatenate([cos_table, sin_table], axis=1))
    qc, qs, pc, ps = contrast_tables(focus, low_y, freq_x, nyquist)
    angle_y, angle_x = turn * low_y[None] * shift_y, turn * freq_x[None] * shift_x
    row_tab = lane_tables([jnp.cos(angle_y), jnp.sin(angle_y), qc, qs], pixels)
    col_tab = jnp.stack([jnp.cos(angle_x), jnp.sin(angle_x), pc, ps], axis=0)

    total_groups = slots // GROUP
    part_groups = total_groups // 4
    parts = [(i * part_groups, part_groups if i < 3 else total_groups - 3 * part_groups) for i in range(4)]
    turned = []
    for start, number in parts:
        turned.append(
            spectra(
                src, patches[0], row_table, col_table, side_table, row_tab, col_tab, start, number
            )
        )
    edge = jnp.concatenate([t[3] for t in turned], axis=1)
    side_re = edge[2, :, :half] - edge[3, :, half:]
    side_im = -(edge[3, :, :half] + edge[2, :, half:])
    side_re = jnp.concatenate([side_re, side_re], axis=1)
    side_im = jnp.concatenate([side_im, -side_im], axis=1)
    side_y = np.concatenate([low_y, -low_y])
    edge_angle = turn * (freq_x[None] * shift_x - float(nyquist) * shift_y)
    side_angle = turn * (side_y[None] * shift_y - float(nyquist) * shift_x)
    edge_cos, edge_sin = jnp.cos(edge_angle), jnp.sin(edge_angle)
    side_cos, side_sin = jnp.cos(side_angle), jnp.sin(side_angle)
    line = jnp.stack(
        [
            edge[0] * edge_cos - edge[1] * edge_sin,
            edge[0] * edge_sin + edge[1] * edge_cos,
            contrast_of(focus[:, None], ((freq_x * freq_x + nyquist * nyquist) * scale_q)[None]),
            side_re * side_cos - side_im * side_sin,
            side_re * side_sin + side_im * side_cos,
            contrast_of(focus[:, None], ((side_y * side_y + nyquist * nyquist) * scale_q)[None]),
        ],
        axis=0,
    )

    since = jnp.where(first, peers - me, me - peers) % owners
    heard = rows_of((since[None, :] == hop_iota[:, None]), heard)
    asked_len = slots + GROUP
    asked_pair = jnp.pad(heard[:, :cap].reshape(-1).astype(jnp.int32), (0, asked_len - used))
    asked_focus = jnp.pad(heard[:, cap : 2 * cap].reshape(-1), (0, asked_len - used))
    far_count = reach - RADIUS
    far_pair = heard[1 : far_count + 1, 2 * cap :].reshape(-1).astype(jnp.int32)

    caps = (cap,) * (far_count - 1) + (cap - share,)
    sent = picked(far_pair, ring_blocks[RADIUS], counts, cap, caps)
    arrived = {}
    for j in range(far_count, 0, -1):
        arrived[RADIUS + j] = lax.ppermute(sent[j - 1], ("dom", "rep"), ring(j))

    aqc, aqs, apc, aps = contrast_tables(asked_focus, low_y, freq_x, nyquist)
    apart = apart_of(
        asked_pair, spreads, counts, lane_tables([aqc, aqs], pixels), jnp.stack([apc, aps], 0)
    )
    apart = jnp.sum(apart, axis=1)

    sums = []
    for (start, number), (re, im, ctf, _) in zip(parts, turned, strict=True):
        begin = start * GROUP // cap
        end = min((start + number) * GROUP // cap, hops)
        sources = [
            (ring_blocks[hop], counts, False) if hop <= RADIUS else ([arrived[hop]], (caps[hop - RADIUS - 1],), True)
            for hop in range(begin, end)
        ]
        rows = line[:, start * GROUP : (start + number) * GROUP]
        sums.append(terms_of(begin, pair_at, sources, (re, im, ctf, rows), cap))

    sums = jnp.concatenate(sums, axis=1)
    inverse_area = 1.0 / (pixels * pixels)
    energy = jnp.sum(sums[0], axis=1)
    grad_x = turn * jnp.sum(freq_x[None] * sums[1] - float(nyquist) * sums[3], axis=1)
    grad_y = turn * jnp.sum(sums[2], axis=1)
    per_slot = jnp.stack(
        [energy * inverse_area, 2.0 * inverse_area * grad_x, 2.0 * inverse_area * grad_y], axis=0
    )
    per_slot = jnp.where(valid[None, :used] > 0.0, per_slot, 0.0)

    spot = tilt_match.astype(jnp.float32)[:used].T[:, None, :]
    node_coef = (spot * per_slot[None, 1:3]).reshape(2 * tilt_dev, used)
    gradient = jnp.dot(
        node_coef,
        weights[:used],
        precision=lax.Precision.HIGHEST,
        preferred_element_type=jnp.float32,
    )
    own_terms = jnp.sum(jnp.where(place[None, :used], per_slot[:, :, None], 0.0), axis=1)
    answers = jnp.pad(apart, (0, node_count // 2 - asked_len))
    rep_row = jnp.arange(2, dtype=jnp.int32)[:, None] == rep
    answers = jnp.where(rep_row, answers[None, :], 0.0)
    gradient, own_terms, answers = lax.psum((gradient, own_terms, answers), "rep")
    bundle = jnp.concatenate([gradient, answers.reshape(1, node_count)], axis=0)
    near = 4
    blocks_of = [[near * i + j for j in range(near)] for i in range(owners // near)]
    strides_of = [[near * i + j for i in range(owners // near)] for j in range(near)]
    here = lax.all_gather(bundle, "dom", axis=0, axis_index_groups=blocks_of)
    bundle = jnp.concatenate(
        [jnp.sum(here[:, : 2 * tilt_dev], axis=0), here[:, 2 * tilt_dev]], axis=0
    )
    everyone = lax.all_gather(bundle, "dom", axis=0, axis_index_groups=strides_of)
    total = jnp.sum(everyone[:, : 2 * tilt_dev], axis=0).reshape(tilt_dev, 2, node_count)
    new_warp = warp_grid - total / jnp.sqrt(total * total + TRUST_FLOOR * TRUST_FLOOR)
    replies = everyone[:, 2 * tilt_dev :].reshape(owners, 2, node_count // 2)
    reply_hop = jnp.arange(node_count // 2, dtype=jnp.int32) // cap
    reply_owner = jnp.stack([me - reply_hop, me + reply_hop], axis=0) % owners
    reply = jnp.sum(jnp.where(peers[:, None, None] == reply_owner[None], replies, 0.0), axis=0)
    reply_lane = jnp.arange(node_count // 2, dtype=jnp.int32)
    reply_hit = (side_of[:, None, None] == jnp.arange(2, dtype=jnp.int32)[None, :, None]) & (
        lane_of[:, None, None] == reply_lane[None, None, :]
    )
    apart_own = jnp.sum(jnp.where(reply_hit, reply[None], 0.0), axis=(1, 2)) * inverse_area
    slot_terms = jnp.concatenate([own_terms[0:1] + apart_own[None], own_terms[1:]], axis=0)
    return (slot_terms[:, None, :], new_warp)


def solution(mesh):
    in_specs = (
        P(("groups", "tilt"), "dom", None, None),
        P(("groups", "tilt"), "dom", None),
        P(("groups", "tilt"), "dom"),
        P(None, ("groups", "tilt"), "dom"),
        P(("groups", "tilt"), "dom"),
        P(("groups", "dom"), "tilt", None, "rep", None),
        P(("groups", "tilt"), None, None),
    )
    out_specs = (P(None, ("groups", "tilt"), "dom"), P(("groups", "tilt"), None, None))

    return jax.shard_map(on_device, mesh=mesh, in_specs=in_specs, out_specs=out_specs, check_vma=False)
```

time: 639 us -> 381 us (0.60)
  the two profiles are of different devices: /device:TPU:33 before, /device:TPU:46 now
where the time goes in v2:
time: 381 us; the launch traced here: 379 us
  starting transfers between devices  122 us (32%)
  waiting for transfers between devices  95.5 us (25%)
  Pallas kernels  69.2 us (18%)
  blocking collectives  55.3 us (15%)
  other arithmetic  18.9 us (5%)
  local copies, waits for them, and re-layouts  15 us (4%)
    ppermute x16, waiting for transfers between devices, on_device(): sent.append(lax.ppermute(block, ('dom', 'rep'), ring(1)))  53.5 us
    all_to_all x1, starting transfers between devices, on_device(): heard = lax.all_to_all(asked, 'dom', 0, 0, tiled=True)  45.8 us
    ppermute x8, starting transfers between devices, on_device(): arrived[RADIUS + j] = lax.ppermute(sent[j - 1], ('dom', 'rep'), ring(j))  39.4 us
    all_gather x1, blocking collectives, on_device(): lax.all_gather(bundle, 'dom', axis=0, axis_index_groups=strides_of)  38.5 us
    ppermute x16, starting transfers between devices, on_device(): sent.append(lax.ppermute(block, ('dom', 'rep'), ring(1)))  34.8 us
    pallas_call x4, Pallas kernels, spectra(): pl.pallas_call(functools.partial(dft_kernel, start=start), grid=(groups,)...  31.4 us
    ppermute x8, waiting for transfers between devices, on_device(): arrived[RADIUS + j] = lax.ppermute(sent[j - 1], ('dom', 'rep'), ring(j))  24 us
    all_to_all x1, waiting for transfers between devices, on_device(): heard = lax.all_to_all(asked, 'dom', 0, 0, tiled=True)  18 us
  transfers between devices with their start and end apart: 26, of which 14 were waited for; matrix products, arithmetic and copies ran while one was open for 7% of the time, Pallas kernels for 15%

profile of v2, /device:TPU:46, one launch (start us, length us, event | category | flops | bytes accessed | tf_op | source)
XLA Modules:
  0.0 378.7 jit_solution(3579388834564774448)
XLA Ops:
  0.6 2.0 collective-permute-start
  8.4 45.8 %all-to-all-start = ((f32[32,1,18]{2,1,0:T(1,128)}), f32[32,1,18]{2,1,0:T(1,128)S(1)}, u32[]{:S(2)}, u32[]{:S(2)}) async-start(f32[32,1,18]{2,1,0:T(1,128)} %copy.45), calls=%async_computation | async-start | bytes 32768 | tf_op jit(solution)/shard_map/all_to_all | solution.py:464
  57.8 18.0 %all-to-all-done = f32[32,1,18]{2,1,0:T(1,128)S(1)} async-done(((f32[32,1,18]{2,1,0:T(1,128)}), f32[32,1,18]{2,1,0:T(1,128)S(1)}, u32[]{:S(2)}, u32[]{:S(2)}) %all-to-all-start) | async-done | bytes 2336 | tf_op jit(solution)/shard_map/all_to_all | solution.py:464
  77.0 0.9 multiply_cosine_fusion.1
  80.6 1.1 copy-done
  81.7 3.9 %fold.2 = (bf16[2640,128]{1,0:T(8,128)(2,1)}, f32[20,64,128]{2,1,0:T(8,128)}) custom-call(s32[1]{0:T(128)} %bitcast.3.rep_ref, bf16[4,10,2,64,128]{4,3,2,1,0:T(8,128)(2,1)} %own_ref.3, bf16[4,10,2,64,128]{4,3,2,1,0:T(8,128)(2,1)} %copy-done), custom_call_target="tpu_custom_call" | custom-call | tf_op jit(solution)/shard_map/fold/pallas_call | solution.py:124
  85.6 1.2 slice.117
  88.0 2.6 collective-permute-start.1
  90.6 3.8 %fold.3 = (bf16[2640,128]{1,0:T(8,128)(2,1)}, f32[20,64,128]{2,1,0:T(8,128)}) custom-call(s32[1]{0:T(128)} %bitcast.3.rep_ref, bf16[4,10,2,64,128]{4,3,2,1,0:T(8,128)(2,1)} %own_ref.3, bf16[4,10,2,64,128]{4,3,2,1,0:T(8,128)(2,1)} %copy-done), custom_call_target="tpu_custom_call" | custom-call | tf_op jit(solution)/shard_map/fold/pallas_call | solution.py:124
  94.4 2.4 collective-permute-start.2
  97.5 4.8 %collective-permute-done.1.refs_2_ = bf16[2640,128]{1,0:T(8,128)(2,1)S(1)} collective-permute-done((bf16[2640,128]{1,0:T(8,128)(2,1)}, bf16[2640,128]{1,0:T(8,128)(2,1)S(1)}, u32[]{:S(2)}, u32[]{:S(2)}) %collective-permute-start.1) | collective-permute-done | bytes 675872 | tf_op jit(solution)/shard_map/ppermute | solution.py:414
  102.3 1.9 collective-permute-start.3
  104.2 5.3 %collective-permute-done.2.refs_3_ = bf16[2640,128]{1,0:T(8,128)(2,1)S(1)} collective-permute-done((bf16[2640,128]{1,0:T(8,128)(2,1)}, bf16[2640,128]{1,0:T(8,128)(2,1)S(1)}, u32[]{:S(2)}, u32[]{:S(2)}) %collective-permute-start.2) | collective-permute-done | bytes 675872 | tf_op jit(solution)/shard_map/ppermute | solution.py:414
  109.5 1.9 collective-permute-start.4
  113.2 3.6 collective-permute-done.3.refs_4_
  116.8 1.9 collective-permute-start.5
  118.7 5.3 %collective-permute-done.4.refs_5_ = bf16[2640,128]{1,0:T(8,128)(2,1)S(1)} collective-permute-done((bf16[2640,128]{1,0:T(8,128)(2,1)S(1)}, bf16[2640,128]{1,0:T(8,128)(2,1)S(1)}, u32[]{:S(2)}, u32[]{:S(2)}) %collective-permute-start.4) | collective-permute-done | bytes 675872 | tf_op jit(solution)/shard_map/ppermute | solution.py:414
  124.0 1.9 collective-permute-start.6
  126.0 9.1 %apart.1 = f32[112,128]{1,0:T(8,128)} custom-call(s32[112]{0:T(128)} %pad.21.ids_ref, f32[20,64,128]{2,1,0:T(8,128)} %get-tuple-element.32.refs_0_, f32[20,64,128]{2,1,0:T(8,128)} %get-tuple-element.57.refs_1_, f32[14,64,128]{2,1,0:T(8,128)} %pad.23.refs_2_, f32[2,112,128]{2,1,0:T(8,128)} %pad_maximum_fusion.2.refs_3_), custom_call_target="tpu_custom_call" | custom-call | flops 1000000000 | bytes 4000000 | tf_op jit(solution)/shard_map/apart/pallas_call | solution.py:336
  135.1 0.9 reduce_sum.205
  137.0 7.5 %spectra.4 = (f32[24,64,128]{2,1,0:T(8,128)}, f32[24,64,128]{2,1,0:T(8,128)}, f32[24,64,128]{2,1,0:T(8,128)}, f32[4,24,128]{2,1,0:T(8,128)}) custom-call(s32[104]{0:T(128)} %get-tuple-element.124.src_ref, bf16[128,128,128]{2,1,0:T(8,128)(2,1)} %bitcast.104, bf16[144,128]{1,0:T(8,128)(2,1)} %constant.169.clone.row_ref, ...), custom_call_target="tpu_custom_call" | custom-call | flops 3000000000 | bytes 20000000 | tf_op jit(solution)/shard_map/spectra/pallas_call | solution.py:179
  144.5 2.0 collective-permute-start.7
  146.4 2.3 collective-permute-start.8
  150.1 7.5 %spectra.6 = (f32[24,64,128]{2,1,0:T(8,128)}, f32[24,64,128]{2,1,0:T(8,128)}, f32[24,64,128]{2,1,0:T(8,128)}, f32[4,24,128]{2,1,0:T(8,128)}) custom-call(s32[104]{0:T(128)} %get-tuple-element.124.src_ref, bf16[128,128,128]{2,1,0:T(8,128)(2,1)} %bitcast.105, bf16[144,128]{1,0:T(8,128)(2,1)} %constant.169.clone.row_ref, ...), custom_call_target="tpu_custom_call" | custom-call | flops 3000000000 | bytes 20000000 | tf_op jit(solution)/shard_map/spectra/pallas_call | solution.py:179
  157.6 7.5 %spectra.5 = (f32[24,64,128]{2,1,0:T(8,128)}, f32[24,64,128]{2,1,0:T(8,128)}, f32[24,64,128]{2,1,0:T(8,128)}, f32[4,24,128]{2,1,0:T(8,128)}) custom-call(s32[104]{0:T(128)} %get-tuple-element.124.src_ref, bf16[128,128,128]{2,1,0:T(8,128)(2,1)} %bitcast.106, bf16[144,128]{1,0:T(8,128)(2,1)} %constant.169.clone.row_ref, ...), custom_call_target="tpu_custom_call" | custom-call | flops 3000000000 | bytes 20000000 | tf_op jit(solution)/shard_map/spectra/pallas_call | solution.py:179
  165.1 3.6 collective-permute-start.9
  168.7 2.1 collective-permute-start.10
  171.7 8.9 %spectra.7 = (f32[32,64,128]{2,1,0:T(8,128)}, f32[32,64,128]{2,1,0:T(8,128)}, f32[32,64,128]{2,1,0:T(8,128)}, f32[4,32,128]{2,1,0:T(8,128)}) custom-call(s32[104]{0:T(128)} %get-tuple-element.124.src_ref, bf16[128,128,128]{2,1,0:T(8,128)(2,1)} %bitcast.107, bf16[144,128]{1,0:T(8,128)(2,1)} %constant.169.clone.row_ref, ...), custom_call_target="tpu_custom_call" | custom-call | flops 4000000000 | bytes 20000000 | tf_op jit(solution)/shard_map/spectra/pallas_call | solution.py:179
  180.7 0.9 constant_dynamic-update-slice_fusion
  181.6 2.0 collective-permute-start.11
  183.6 2.7 collective-permute-done.10.refs_3_
  186.3 2.4 collective-permute-start.12
  189.4 6.1 %collective-permute-done.11.refs_4_ = bf16[2640,128]{1,0:T(8,128)(2,1)S(1)} collective-permute-done((bf16[2640,128]{1,0:T(8,128)(2,1)S(1)}, bf16[2640,128]{1,0:T(8,128)(2,1)S(1)}, u32[]{:S(2)}, u32[]{:S(2)}) %collective-permute-start.11) | collective-permute-done | bytes 675872 | tf_op jit(solution)/shard_map/ppermute | solution.py:414
  195.5 1.9 collective-permute-start.13
  197.5 5.3 %collective-permute-done.12.refs_5_ = bf16[2640,128]{1,0:T(8,128)(2,1)S(1)} collective-permute-done((bf16[2640,128]{1,0:T(8,128)(2,1)S(1)}, bf16[2640,128]{1,0:T(8,128)(2,1)S(1)}, u32[]{:S(2)}, u32[]{:S(2)}) %collective-permute-start.12) | collective-permute-done | bytes 675872 | tf_op jit(solution)/shard_map/ppermute | solution.py:414
  202.8 1.9 collective-permute-start.14
  205.6 4.4 %collective-permute-done.13.refs_6_ = bf16[2640,128]{1,0:T(8,128)(2,1)S(1)} collective-permute-done((bf16[2640,128]{1,0:T(8,128)(2,1)S(1)}, bf16[2640,128]{1,0:T(8,128)(2,1)S(1)}, u32[]{:S(2)}, u32[]{:S(2)}) %collective-permute-start.13) | collective-permute-done | bytes 675872 | tf_op jit(solution)/shard_map/ppermute | solution.py:414
  210.0 1.9 collective-permute-start.15
  211.9 5.3 %collective-permute-done.14.refs_7_ = bf16[2640,128]{1,0:T(8,128)(2,1)S(1)} collective-permute-done((bf16[2640,128]{1,0:T(8,128)(2,1)S(1)}, bf16[2640,128]{1,0:T(8,128)(2,1)S(1)}, u32[]{:S(2)}, u32[]{:S(2)}) %collective-permute-start.14) | collective-permute-done | bytes 675872 | tf_op jit(solution)/shard_map/ppermute | solution.py:414
  217.2 1.9 collective-permute-start.16
  219.2 0.9 fusion.26
  220.9 3.6 collective-permute-done.15.refs_0_
  224.5 7.2 %collective-permute-done.16.refs_1_ = bf16[2640,128]{1,0:T(8,128)(2,1)S(1)} collective-permute-done((bf16[2640,128]{1,0:T(8,128)(2,1)S(1)}, bf16[2640,128]{1,0:T(8,128)(2,1)S(1)}, u32[]{:S(2)}, u32[]{:S(2)}) %collective-permute-start.16) | collective-permute-done | bytes 675872 | tf_op jit(solution)/shard_map/ppermute | solution.py:414
  231.7 0.9 copy-done.2
  232.6 3.6 pick.1
  236.2 1.9 collective-permute-start.17
  238.1 2.5 collective-permute-start.18
  240.7 2.6 collective-permute-start.19
  244.1 1.5 slice.162.refs_8_
  245.6 2.6 collective-permute-start.20
  248.3 7.2 %collective-permute-start.21 = (bf16[800,128]{1,0:T(8,128)(2,1)}, bf16[800,128]{1,0:T(8,128)(2,1)S(1)}, u32[]{:S(2)}, u32[]{:S(2)}) collective-permute-start(bf16[800,128]{1,0:T(8,128)(2,1)} %get-tuple-element.50), channel_id=1, source_target_pairs={{0,40},{1,217},{8,48},{9,225},{16,56},{17,233},{24,64},{25,241},{3... | collective-permute-start | bytes 614408 | tf_op jit(solution)/shard_map/ppermute | solution.py:537
  255.5 8.1 %collective-permute-start.22 = (bf16[800,128]{1,0:T(8,128)(2,1)}, bf16[800,128]{1,0:T(8,128)(2,1)S(1)}, u32[]{:S(2)}, u32[]{:S(2)}) collective-permute-start(bf16[800,128]{1,0:T(8,128)(2,1)} %get-tuple-element.51), channel_id=1, source_target_pairs={{0,48},{1,209},{8,56},{9,217},{16,64},{17,225},{24,72},{25,233},{3... | collective-permute-start | bytes 614408 | tf_op jit(solution)/shard_map/ppermute | solution.py:537
  263.6 12.0 %collective-permute-start.23 = (bf16[800,128]{1,0:T(8,128)(2,1)}, bf16[800,128]{1,0:T(8,128)(2,1)S(1)}, u32[]{:S(2)}, u32[]{:S(2)}) collective-permute-start(bf16[800,128]{1,0:T(8,128)(2,1)} %get-tuple-element.52), channel_id=1, source_target_pairs={{0,56},{1,201},{8,64},{9,209},{16,72},{17,217},{24,80},{25,225},{3... | collective-permute-start | bytes 614408 | tf_op jit(solution)/shard_map/ppermute | solution.py:537
  275.6 5.0 %terms.4 = f32[4,24,128]{2,1,0:T(8,128)} custom-call(s32[104]{0:T(128)} %copy-done.33, bf16[2640,128]{1,0:T(8,128)(2,1)} %get-tuple-element.30.refs_0_, bf16[2640,128]{1,0:T(8,128)(2,1)} %get-tuple-element.31.refs_1_, bf16[2640,128]{1,0:T(8,128)(2,1)} %copy-done.3, bf16[2640,128]{1,0:T(8,128)(2,1)} %copy-done.4, bf16[2640,128]{1,0:T(8,128)(2,1)} %copy-done.5, ...), custom_call_target="tpu_custom_call" | custom-call | flops 1000000000 | bytes 10000000 | tf_op jit(solution)/shard_map/terms/pallas_call | solution.py:266
  280.6 2.4 collective-permute-start.24
  283.0 5.1 %terms.5 = f32[4,24,128]{2,1,0:T(8,128)} custom-call(s32[104]{0:T(128)} %copy-done.33, bf16[2640,128]{1,0:T(8,128)(2,1)} %copy-done.7, bf16[2640,128]{1,0:T(8,128)(2,1)} %copy-done.8, bf16[2640,128]{1,0:T(8,128)(2,1)} %copy-done.9, bf16[2640,128]{1,0:T(8,128)(2,1)} %copy-done.10, bf16[2640,128]{1,0:T(8,128)(2,1)} %copy-done.11, ...), custom_call_target="tpu_custom_call" | custom-call | flops 1000000000 | bytes 10000000 | tf_op jit(solution)/shard_map/terms/pallas_call | solution.py:266
  288.1 3.6 terms.6
  291.8 22.9 %collective-permute-done.24.refs_4_ = bf16[400,128]{1,0:T(8,128)(2,1)S(1)} collective-permute-done((bf16[400,128]{1,0:T(8,128)(2,1)S(1)}, bf16[400,128]{1,0:T(8,128)(2,1)S(1)}, u32[]{:S(2)}, u32[]{:S(2)}) %collective-permute-start.24) | collective-permute-done | bytes 102432 | tf_op jit(solution)/shard_map/ppermute | solution.py:537
  314.7 1.1 collective-permute-done.23.refs_3_
  316.5 3.7 terms.7
  320.2 0.9 pad_maximum_fusion.1
  321.8 3.5 all-reduce.5
  325.3 13.3 %all-gather.2 = f32[4,21,256]{2,1,0:T(8,128)S(1)} all-gather(f32[1,21,256]{2,1,0:T(8,128)S(1)} %maximum_bitcast_fusion.2), channel_id=2, replica_groups={{0,8,16,24},{32,40,48,56},{64,72,80,88},{96,104,112,120},{128,136,144,1..., dimensions={0}, use_global_device_ids=true | all-gather | bytes 107520 | tf_op jit(solution)/shard_map/all_gather | solution.py:583
  338.6 38.5 %all-gather.1 = f32[192,256]{1,0:T(8,128)S(1)} all-gather(f32[24,256]{1,0:T(8,128)S(1)} %pad_maximum_fusion.5), channel_id=3, replica_groups={{0,32,64,96,128,160,192,224},{8,40,72,104,136,168,200,232},{16,48,80,11..., dimensions={0}, use_global_device_ids=true | all-gather | bytes 221184 | tf_op jit(solution)/shard_map/all_gather | solution.py:587
  (208 shorter events, 25.3 us)
Async XLA Ops:
  0.6 79.0 %copy-start.39 = (f32[128]{0:T(128)S(1)}, f32[128]{0:T(128)}, u32[]{:S(2)}) copy-start(f32[128]{0:T(128)} %constant.200) | copy-start | bytes 1540
  0.6 80.0 %collective-permute-start = (bf16[4,10,2,64,128]{4,3,2,1,0:T(8,128)(2,1)}, bf16[4,10,2,64,128]{4,3,2,1,0:T(8,128)(2,1)S(1)}, u32[]{:S(2)}, u32[]{:S(2)}) collective-permute-start(bf16[4,10,2,64,128]{4,3,2,1,0:T(8,128)(2,1)} %own_ref.3), channel_id=1, source_target_pairs={{0,1},{1,0},{2,3},{3,2},{4,5},{5,4},{6,7},{7,6},{8,9},{9,8},{10,11... | collective-permute-start | bytes 3932168 | tf_op jit(solution)/shard_map/ppermute | solution.py:395
  8.4 67.5 %all-to-all-start = ((f32[32,1,18]{2,1,0:T(1,128)}), f32[32,1,18]{2,1,0:T(1,128)S(1)}, u32[]{:S(2)}, u32[]{:S(2)}) async-start(f32[32,1,18]{2,1,0:T(1,128)} %copy.45), calls=%async_computation | async-start | bytes 32768 | tf_op jit(solution)/shard_map/all_to_all | solution.py:464
  88.0 9.0 %copy-start.30 = (pred[104,10]{0,1:T(8,128)(4,1)}, pred[104,10]{0,1:T(8,128)(4,1)S(1)}, u32[]{:S(2)}) copy-start(pred[104,10]{0,1:T(8,128)(4,1)S(1)} %iota_compare_fusion.6) | copy-start | bytes 3124
  88.0 9.1 %copy-start.26 = (f32[10,2,256]{2,1,0:T(2,128)S(1)}, f32[10,2,256]{2,1,0:T(2,128)}, u32[]{:S(2)}) copy-start(f32[10,2,256]{2,1,0:T(2,128)} %param.27) | copy-start | bytes 61444
  88.0 9.3 %copy-start.40 = (f32[64]{0:T(128)S(1)}, f32[64]{0:T(128)}, u32[]{:S(2)}) copy-start(f32[64]{0:T(128)} %constant.198) | copy-start | bytes 772
  88.0 23.6 %copy-start.44 = (f32[64]{0:T(128)S(1)}, f32[64]{0:T(128)}, u32[]{:S(2)}) copy-start(f32[64]{0:T(128)} %constant.197) | copy-start | bytes 772
  88.0 14.3 %collective-permute-start.1 = (bf16[2640,128]{1,0:T(8,128)(2,1)}, bf16[2640,128]{1,0:T(8,128)(2,1)S(1)}, u32[]{:S(2)}, u32[]{:S(2)}) collective-permute-start(bf16[2640,128]{1,0:T(8,128)(2,1)} %get-tuple-element.30.refs_0_), channel_id=1, source_target_pairs={{0,8},{1,249},{8,16},{9,1},{16,24},{17,9},{24,32},{25,17},{32,40},... | collective-permute-start | bytes 2027528 | tf_op jit(solution)/shard_map/ppermute | solution.py:414
  94.4 15.1 %collective-permute-start.2 = (bf16[2640,128]{1,0:T(8,128)(2,1)}, bf16[2640,128]{1,0:T(8,128)(2,1)S(1)}, u32[]{:S(2)}, u32[]{:S(2)}) collective-permute-start(bf16[2640,128]{1,0:T(8,128)(2,1)} %get-tuple-element.31.refs_1_), channel_id=1, source_target_pairs={{0,8},{1,249},{8,16},{9,1},{16,24},{17,9},{24,32},{25,17},{32,40},... | collective-permute-start | bytes 2027528 | tf_op jit(solution)/shard_map/ppermute | solution.py:414
  96.9 107.8 %copy-start.36 = (f32[104]{0:T(128)}, f32[104]{0:T(128)S(1)}, u32[]{:S(2)}) copy-start(f32[104]{0:T(128)S(1)} %get-tuple-element.115) | copy-start | bytes 1252
  102.3 32.8 %copy-start.3 = (bf16[2640,128]{1,0:T(8,128)(2,1)}, bf16[2640,128]{1,0:T(8,128)(2,1)S(1)}, u32[]{:S(2)}) copy-start(bf16[2640,128]{1,0:T(8,128)(2,1)S(1)} %collective-permute-done.1.refs_2_) | copy-start | bytes 2027524
  102.3 14.5 %collective-permute-start.3 = (bf16[2640,128]{1,0:T(8,128)(2,1)S(1)}, bf16[2640,128]{1,0:T(8,128)(2,1)S(1)}, u32[]{:S(2)}, u32[]{:S(2)}) collective-permute-start(bf16[2640,128]{1,0:T(8,128)(2,1)S(1)} %collective-permute-done.1.refs_2_), channel_id=1, source_target_pairs={{0,8},{1,249},{8,16},{9,1},{16,24},{17,9},{24,32},{25,17},{32,40},... | collective-permute-start | bytes 2027528 | tf_op jit(solution)/shard_map/ppermute | solution.py:414
  109.5 25.5 %copy-start.4 = (bf16[2640,128]{1,0:T(8,128)(2,1)}, bf16[2640,128]{1,0:T(8,128)(2,1)S(1)}, u32[]{:S(2)}) copy-start(bf16[2640,128]{1,0:T(8,128)(2,1)S(1)} %collective-permute-done.2.refs_3_) | copy-start | bytes 2027524
  109.5 14.5 %collective-permute-start.4 = (bf16[2640,128]{1,0:T(8,128)(2,1)S(1)}, bf16[2640,128]{1,0:T(8,128)(2,1)S(1)}, u32[]{:S(2)}, u32[]{:S(2)}) collective-permute-start(bf16[2640,128]{1,0:T(8,128)(2,1)S(1)} %collective-permute-done.2.refs_3_), channel_id=1, source_target_pairs={{0,8},{1,249},{8,16},{9,1},{16,24},{17,9},{24,32},{25,17},{32,40},... | collective-permute-start | bytes 2027528 | tf_op jit(solution)/shard_map/ppermute | solution.py:414
  116.8 18.3 %copy-start.5 = (bf16[2640,128]{1,0:T(8,128)(2,1)}, bf16[2640,128]{1,0:T(8,128)(2,1)S(1)}, u32[]{:S(2)}) copy-start(bf16[2640,128]{1,0:T(8,128)(2,1)S(1)} %collective-permute-done.3.refs_4_) | copy-start | bytes 2027524
  116.8 27.7 %collective-permute-start.5 = (bf16[2640,128]{1,0:T(8,128)(2,1)S(1)}, bf16[2640,128]{1,0:T(8,128)(2,1)}, u32[]{:S(2)}, u32[]{:S(2)}) collective-permute-start(bf16[2640,128]{1,0:T(8,128)(2,1)S(1)} %collective-permute-done.3.refs_4_), channel_id=1, source_target_pairs={{0,8},{1,249},{8,16},{9,1},{16,24},{17,9},{24,32},{25,17},{32,40},... | collective-permute-start | bytes 2027528 | tf_op jit(solution)/shard_map/ppermute | solution.py:414
  124.0 11.1 %copy-start.6 = (bf16[2640,128]{1,0:T(8,128)(2,1)}, bf16[2640,128]{1,0:T(8,128)(2,1)S(1)}, u32[]{:S(2)}) copy-start(bf16[2640,128]{1,0:T(8,128)(2,1)S(1)} %collective-permute-done.4.refs_5_) | copy-start | bytes 2027524
  124.0 22.4 %collective-permute-start.6 = (bf16[2640,128]{1,0:T(8,128)(2,1)S(1)}, bf16[2640,128]{1,0:T(8,128)(2,1)}, u32[]{:S(2)}, u32[]{:S(2)}) collective-permute-start(bf16[2640,128]{1,0:T(8,128)(2,1)S(1)} %collective-permute-done.4.refs_5_), channel_id=1, source_target_pairs={{0,8},{1,249},{8,16},{9,1},{16,24},{17,9},{24,32},{25,17},{32,40},... | collective-permute-start | bytes 2027528 | tf_op jit(solution)/shard_map/ppermute | solution.py:414
  126.0 10.0 %copy-start.43 = (f32[128]{0:T(128)S(1)}, f32[128]{0:T(128)}, u32[]{:S(2)}) copy-start(f32[128]{0:T(128)} %constant.199) | copy-start | bytes 1540
  144.5 20.6 %collective-permute-start.7 = (bf16[2640,128]{1,0:T(8,128)(2,1)}, bf16[2640,128]{1,0:T(8,128)(2,1)S(1)}, u32[]{:S(2)}, u32[]{:S(2)}) collective-permute-start(bf16[2640,128]{1,0:T(8,128)(2,1)} %collective-permute-done.5.refs_6_), channel_id=1, source_target_pairs={{0,8},{1,249},{8,16},{9,1},{16,24},{17,9},{24,32},{25,17},{32,40},... | collective-permute-start | bytes 2027528 | tf_op jit(solution)/shard_map/ppermute | solution.py:414
  146.4 22.3 %collective-permute-start.8 = (bf16[2640,128]{1,0:T(8,128)(2,1)}, bf16[2640,128]{1,0:T(8,128)(2,1)S(1)}, u32[]{:S(2)}, u32[]{:S(2)}) collective-permute-start(bf16[2640,128]{1,0:T(8,128)(2,1)} %collective-permute-done.6.refs_7_), channel_id=1, source_target_pairs={{0,8},{1,249},{8,16},{9,1},{16,24},{17,9},{24,32},{25,17},{32,40},... | collective-permute-start | bytes 2027528 | tf_op jit(solution)/shard_map/ppermute | solution.py:414
  157.6 14.1 %copy-start.29 = (f32[4,24,128]{2,1,0:T(8,128)S(1)}, f32[4,24,128]{2,1,0:T(8,128)}, u32[]{:S(2)}) copy-start(f32[4,24,128]{2,1,0:T(8,128)} %get-tuple-element.38) | copy-start | bytes 147460
  165.1 15.6 %copy-start.7 = (bf16[2640,128]{1,0:T(8,128)(2,1)}, bf16[2640,128]{1,0:T(8,128)(2,1)S(1)}, u32[]{:S(2)}) copy-start(bf16[2640,128]{1,0:T(8,128)(2,1)S(1)} %collective-permute-done.7.refs_0_) | copy-start | bytes 2027524
  165.1 16.4 %collective-permute-start.9 = (bf16[2640,128]{1,0:T(8,128)(2,1)S(1)}, bf16[2640,128]{1,0:T(8,128)(2,1)S(1)}, u32[]{:S(2)}, u32[]{:S(2)}) collective-permute-start(bf16[2640,128]{1,0:T(8,128)(2,1)S(1)} %collective-permute-done.7.refs_0_), channel_id=1, source_target_pairs={{0,8},{1,249},{8,16},{9,1},{16,24},{17,9},{24,32},{25,17},{32,40},... | collective-permute-start | bytes 2027528 | tf_op jit(solution)/shard_map/ppermute | solution.py:414
  168.7 12.0 %copy-start.8 = (bf16[2640,128]{1,0:T(8,128)(2,1)}, bf16[2640,128]{1,0:T(8,128)(2,1)S(1)}, u32[]{:S(2)}) copy-start(bf16[2640,128]{1,0:T(8,128)(2,1)S(1)} %collective-permute-done.8.refs_1_) | copy-start | bytes 2027524
  168.7 17.6 %collective-permute-start.10 = (bf16[2640,128]{1,0:T(8,128)(2,1)S(1)}, bf16[2640,128]{1,0:T(8,128)(2,1)S(1)}, u32[]{:S(2)}, u32[]{:S(2)}) collective-permute-start(bf16[2640,128]{1,0:T(8,128)(2,1)S(1)} %collective-permute-done.8.refs_1_), channel_id=1, source_target_pairs={{0,8},{1,249},{8,16},{9,1},{16,24},{17,9},{24,32},{25,17},{32,40},... | collective-permute-start | bytes 2027528 | tf_op jit(solution)/shard_map/ppermute | solution.py:414
  171.7 17.0 %copy-start.34 = (f32[128]{0:T(128)S(1)}, f32[128]{0:T(128)}, u32[]{:S(2)}) copy-start(f32[128]{0:T(128)} %constant.201) | copy-start | bytes 1540
  171.7 33.0 %copy-start.42 = (f32[128]{0:T(128)S(1)}, f32[128]{0:T(128)}, u32[]{:S(2)}) copy-start(f32[128]{0:T(128)} %constant.202) | copy-start | bytes 1540
  171.7 33.3 %copy-start.38 = (f32[128]{0:T(128)S(1)}, f32[128]{0:T(128)}, u32[]{:S(2)}) copy-start(f32[128]{0:T(128)} %constant.203) | copy-start | bytes 1540
  180.7 38.5 %copy-start.31 = (pred[104,10]{0,1:T(8,128)(4,1)S(1)}, pred[104,10]{0,1:T(8,128)(4,1)}, u32[]{:S(2)}) copy-start(pred[104,10]{0,1:T(8,128)(4,1)} %copy-done.30) | copy-start | bytes 3124
  180.7 38.5 %copy-start.41 = (f32[128]{0:T(128)S(1)}, f32[128]{0:T(128)}, u32[]{:S(2)}) copy-start(f32[128]{0:T(128)} %constant.204) | copy-start | bytes 1540
  181.6 54.6 %copy-start.9 = (bf16[2640,128]{1,0:T(8,128)(2,1)}, bf16[2640,128]{1,0:T(8,128)(2,1)S(1)}, u32[]{:S(2)}) copy-start(bf16[2640,128]{1,0:T(8,128)(2,1)S(1)} %collective-permute-done.9.refs_2_) | copy-start | bytes 2027524
  181.6 13.9 %collective-permute-start.11 = (bf16[2640,128]{1,0:T(8,128)(2,1)S(1)}, bf16[2640,128]{1,0:T(8,128)(2,1)S(1)}, u32[]{:S(2)}, u32[]{:S(2)}) collective-permute-start(bf16[2640,128]{1,0:T(8,128)(2,1)S(1)} %collective-permute-done.9.refs_2_), channel_id=1, source_target_pairs={{0,8},{1,249},{8,16},{9,1},{16,24},{17,9},{24,32},{25,17},{32,40},... | collective-permute-start | bytes 2027528 | tf_op jit(solution)/shard_map/ppermute | solution.py:414
  186.3 19.3 %copy-start.10 = (bf16[2640,128]{1,0:T(8,128)(2,1)}, bf16[2640,128]{1,0:T(8,128)(2,1)S(1)}, u32[]{:S(2)}) copy-start(bf16[2640,128]{1,0:T(8,128)(2,1)S(1)} %collective-permute-done.10.refs_3_) | copy-start | bytes 2027524
  186.3 16.4 %collective-permute-start.12 = (bf16[2640,128]{1,0:T(8,128)(2,1)S(1)}, bf16[2640,128]{1,0:T(8,128)(2,1)S(1)}, u32[]{:S(2)}, u32[]{:S(2)}) collective-permute-start(bf16[2640,128]{1,0:T(8,128)(2,1)S(1)} %collective-permute-done.10.refs_3_), channel_id=1, source_target_pairs={{0,8},{1,249},{8,16},{9,1},{16,24},{17,9},{24,32},{25,17},{32,40},... | collective-permute-start | bytes 2027528 | tf_op jit(solution)/shard_map/ppermute | solution.py:414
  195.5 85.1 %copy-start.11 = (bf16[2640,128]{1,0:T(8,128)(2,1)}, bf16[2640,128]{1,0:T(8,128)(2,1)S(1)}, u32[]{:S(2)}) copy-start(bf16[2640,128]{1,0:T(8,128)(2,1)S(1)} %collective-permute-done.11.refs_4_) | copy-start | bytes 2027524
  195.5 14.5 %collective-permute-start.13 = (bf16[2640,128]{1,0:T(8,128)(2,1)S(1)}, bf16[2640,128]{1,0:T(8,128)(2,1)S(1)}, u32[]{:S(2)}, u32[]{:S(2)}) collective-permute-start(bf16[2640,128]{1,0:T(8,128)(2,1)S(1)} %collective-permute-done.11.refs_4_), channel_id=1, source_target_pairs={{0,8},{1,249},{8,16},{9,1},{16,24},{17,9},{24,32},{25,17},{32,40},... | collective-permute-start | bytes 2027528 | tf_op jit(solution)/shard_map/ppermute | solution.py:414
  202.8 77.8 %copy-start.12 = (bf16[2640,128]{1,0:T(8,128)(2,1)}, bf16[2640,128]{1,0:T(8,128)(2,1)S(1)}, u32[]{:S(2)}) copy-start(bf16[2640,128]{1,0:T(8,128)(2,1)S(1)} %collective-permute-done.12.refs_5_) | copy-start | bytes 2027524
  202.8 14.5 %collective-permute-start.14 = (bf16[2640,128]{1,0:T(8,128)(2,1)S(1)}, bf16[2640,128]{1,0:T(8,128)(2,1)S(1)}, u32[]{:S(2)}, u32[]{:S(2)}) collective-permute-start(bf16[2640,128]{1,0:T(8,128)(2,1)S(1)} %collective-permute-done.12.refs_5_), channel_id=1, source_target_pairs={{0,8},{1,249},{8,16},{9,1},{16,24},{17,9},{24,32},{25,17},{32,40},... | collective-permute-start | bytes 2027528 | tf_op jit(solution)/shard_map/ppermute | solution.py:414
  210.0 14.5 %copy-start.13 = (bf16[2640,128]{1,0:T(8,128)(2,1)}, bf16[2640,128]{1,0:T(8,128)(2,1)S(1)}, u32[]{:S(2)}) copy-start(bf16[2640,128]{1,0:T(8,128)(2,1)S(1)} %collective-permute-done.13.refs_6_) | copy-start | bytes 2027524
  210.0 14.5 %collective-permute-start.15 = (bf16[2640,128]{1,0:T(8,128)(2,1)S(1)}, bf16[2640,128]{1,0:T(8,128)(2,1)S(1)}, u32[]{:S(2)}, u32[]{:S(2)}) collective-permute-start(bf16[2640,128]{1,0:T(8,128)(2,1)S(1)} %collective-permute-done.13.refs_6_), channel_id=1, source_target_pairs={{0,8},{1,249},{8,16},{9,1},{16,24},{17,9},{24,32},{25,17},{32,40},... | collective-permute-start | bytes 2027528 | tf_op jit(solution)/shard_map/ppermute | solution.py:414
  217.2 7.2 %copy-start.14 = (bf16[2640,128]{1,0:T(8,128)(2,1)}, bf16[2640,128]{1,0:T(8,128)(2,1)S(1)}, u32[]{:S(2)}) copy-start(bf16[2640,128]{1,0:T(8,128)(2,1)S(1)} %collective-permute-done.14.refs_7_) | copy-start | bytes 2027524
  217.2 14.5 %collective-permute-start.16 = (bf16[2640,128]{1,0:T(8,128)(2,1)S(1)}, bf16[2640,128]{1,0:T(8,128)(2,1)S(1)}, u32[]{:S(2)}, u32[]{:S(2)}) collective-permute-start(bf16[2640,128]{1,0:T(8,128)(2,1)S(1)} %collective-permute-done.14.refs_7_), channel_id=1, source_target_pairs={{0,8},{1,249},{8,16},{9,1},{16,24},{17,9},{24,32},{25,17},{32,40},... | collective-permute-start | bytes 2027528 | tf_op jit(solution)/shard_map/ppermute | solution.py:414
  220.2 4.3 %copy-start.15 = (f32[6,104,128]{2,1,0:T(8,128)}, f32[6,104,128]{2,1,0:T(8,128)S(1)}, u32[]{:S(2)}) copy-start(f32[6,104,128]{2,1,0:T(8,128)S(1)} %fusion.26) | copy-start | bytes 958468
  224.5 7.2 %copy-start.1 = (bf16[2640,128]{1,0:T(8,128)(2,1)}, bf16[2640,128]{1,0:T(8,128)(2,1)S(1)}, u32[]{:S(2)}) copy-start(bf16[2640,128]{1,0:T(8,128)(2,1)S(1)} %collective-permute-done.15.refs_0_) | copy-start | bytes 2027524
  236.2 19.2 %collective-permute-start.17 = (bf16[800,128]{1,0:T(8,128)(2,1)}, bf16[800,128]{1,0:T(8,128)(2,1)S(1)}, u32[]{:S(2)}, u32[]{:S(2)}) collective-permute-start(bf16[800,128]{1,0:T(8,128)(2,1)} %get-tuple-element.43), channel_id=1, source_target_pairs={{0,8},{1,249},{8,16},{9,1},{16,24},{17,9},{24,32},{25,17},{32,40},... | collective-permute-start | bytes 614408 | tf_op jit(solution)/shard_map/ppermute | solution.py:537
  238.1 25.4 %collective-permute-start.18 = (bf16[800,128]{1,0:T(8,128)(2,1)}, bf16[800,128]{1,0:T(8,128)(2,1)S(1)}, u32[]{:S(2)}, u32[]{:S(2)}) collective-permute-start(bf16[800,128]{1,0:T(8,128)(2,1)} %get-tuple-element.44), channel_id=1, source_target_pairs={{0,16},{1,241},{8,24},{9,249},{16,32},{17,1},{24,40},{25,9},{32,48... | collective-permute-start | bytes 614408 | tf_op jit(solution)/shard_map/ppermute | solution.py:537
  240.7 39.9 %collective-permute-start.19 = (bf16[800,128]{1,0:T(8,128)(2,1)}, bf16[800,128]{1,0:T(8,128)(2,1)S(1)}, u32[]{:S(2)}, u32[]{:S(2)}) collective-permute-start(bf16[800,128]{1,0:T(8,128)(2,1)} %get-tuple-element.45), channel_id=1, source_target_pairs={{0,24},{1,233},{8,32},{9,241},{16,40},{17,249},{24,48},{25,1},{32,... | collective-permute-start | bytes 614408 | tf_op jit(solution)/shard_map/ppermute | solution.py:537
  245.6 69.0 %collective-permute-start.20 = (bf16[800,128]{1,0:T(8,128)(2,1)}, bf16[800,128]{1,0:T(8,128)(2,1)S(1)}, u32[]{:S(2)}, u32[]{:S(2)}) collective-permute-start(bf16[800,128]{1,0:T(8,128)(2,1)} %get-tuple-element.49), channel_id=1, source_target_pairs={{0,32},{1,225},{8,40},{9,233},{16,48},{17,241},{24,56},{25,249},{3... | collective-permute-start | bytes 614408 | tf_op jit(solution)/shard_map/ppermute | solution.py:537
  248.3 66.4 %collective-permute-start.21 = (bf16[800,128]{1,0:T(8,128)(2,1)}, bf16[800,128]{1,0:T(8,128)(2,1)S(1)}, u32[]{:S(2)}, u32[]{:S(2)}) collective-permute-start(bf16[800,128]{1,0:T(8,128)(2,1)} %get-tuple-element.50), channel_id=1, source_target_pairs={{0,40},{1,217},{8,48},{9,225},{16,56},{17,233},{24,64},{25,241},{3... | collective-permute-start | bytes 614408 | tf_op jit(solution)/shard_map/ppermute | solution.py:537
  255.4 25.2 %copy-start.19 = (bf16[800,128]{1,0:T(8,128)(2,1)}, bf16[800,128]{1,0:T(8,128)(2,1)S(1)}, u32[]{:S(2)}) copy-start(bf16[800,128]{1,0:T(8,128)(2,1)S(1)} %collective-permute-done.17.refs_2_) | copy-start | bytes 614404
  255.5 59.2 %collective-permute-start.22 = (bf16[800,128]{1,0:T(8,128)(2,1)}, bf16[800,128]{1,0:T(8,128)(2,1)S(1)}, u32[]{:S(2)}, u32[]{:S(2)}) collective-permute-start(bf16[800,128]{1,0:T(8,128)(2,1)} %get-tuple-element.51), channel_id=1, source_target_pairs={{0,48},{1,209},{8,56},{9,217},{16,64},{17,225},{24,72},{25,233},{3... | collective-permute-start | bytes 614408 | tf_op jit(solution)/shard_map/ppermute | solution.py:537
  263.5 17.1 %copy-start.20 = (bf16[800,128]{1,0:T(8,128)(2,1)}, bf16[800,128]{1,0:T(8,128)(2,1)S(1)}, u32[]{:S(2)}) copy-start(bf16[800,128]{1,0:T(8,128)(2,1)S(1)} %collective-permute-done.18.refs_3_) | copy-start | bytes 614404
  263.6 52.2 %collective-permute-start.23 = (bf16[800,128]{1,0:T(8,128)(2,1)}, bf16[800,128]{1,0:T(8,128)(2,1)S(1)}, u32[]{:S(2)}, u32[]{:S(2)}) collective-permute-start(bf16[800,128]{1,0:T(8,128)(2,1)} %get-tuple-element.52), channel_id=1, source_target_pairs={{0,56},{1,201},{8,64},{9,209},{16,72},{17,217},{24,80},{25,225},{3... | collective-permute-start | bytes 614408 | tf_op jit(solution)/shard_map/ppermute | solution.py:537
  275.6 5.1 %copy-start.47 = (bf16[400,128]{1,0:T(8,128)(2,1)S(1)}, bf16[400,128]{1,0:T(8,128)(2,1)}, u32[]{:S(2)}) copy-start(bf16[400,128]{1,0:T(8,128)(2,1)} %get-tuple-element.53) | copy-start | bytes 307204
  280.6 7.5 %copy-start.22 = (bf16[800,128]{1,0:T(8,128)(2,1)}, bf16[800,128]{1,0:T(8,128)(2,1)S(1)}, u32[]{:S(2)}) copy-start(bf16[800,128]{1,0:T(8,128)(2,1)S(1)} %collective-permute-done.19.refs_4_) | copy-start | bytes 614404
  280.6 34.0 %collective-permute-start.24 = (bf16[400,128]{1,0:T(8,128)(2,1)S(1)}, bf16[400,128]{1,0:T(8,128)(2,1)S(1)}, u32[]{:S(2)}, u32[]{:S(2)}) collective-permute-start(bf16[400,128]{1,0:T(8,128)(2,1)S(1)} %copy-done.47), channel_id=1, source_target_pairs={{0,64},{1,193},{8,72},{9,201},{16,80},{17,209},{24,88},{25,217},{3... | collective-permute-start | bytes 307208 | tf_op jit(solution)/shard_map/ppermute | solution.py:537
  316.5 3.7 copy-start.25
  316.5 4.7 %copy-start.35 = (f32[128]{0:T(128)S(1)}, f32[128]{0:T(128)}, u32[]{:S(2)}) copy-start(f32[128]{0:T(128)} %constant.201) | copy-start | bytes 1540
  316.5 4.9 %copy-start.46 = (pred[102]{0:T(512)(128)(4,1)S(1)}, pred[102]{0:T(512)(128)(4,1)}, u32[]{:S(2)}) copy-start(pred[102]{0:T(512)(128)(4,1)} %fusion.42) | copy-start | bytes 310
  316.5 4.9 %copy-start.28 = (pred[104,128]{1,0:T(8,128)(4,1)S(1)}, pred[104,128]{1,0:T(8,128)(4,1)}, u32[]{:S(2)}) copy-start(pred[104,128]{1,0:T(8,128)(4,1)} %get-tuple-element.104) | copy-start | bytes 39940
  320.2 57.6 %copy-start.32 = (s32[8,4]{1,0:T(8,128)S(1)}, s32[8,4]{1,0:T(8,128)}, u32[]{:S(2)}) copy-start(s32[8,4]{1,0:T(8,128)} %multiply_add_fusion) | copy-start | bytes 388
  320.2 57.6 %copy-start.37 = (s32[256]{0:T(256)S(1)}, s32[256]{0:T(256)}, u32[]{:S(2)}) copy-start(s32[256]{0:T(256)} %and_select_fusion) | copy-start | bytes 3076
  320.2 57.7 %copy-start.45 = (pred[128,2]{0,1:T(4,128)(4,1)S(1)}, pred[128,2]{0,1:T(4,128)(4,1)}, u32[]{:S(2)}) copy-start(pred[128,2]{0,1:T(4,128)(4,1)} %iota_compare_fusion.7) | copy-start | bytes 772
  (10 other events, 15.2 us)

commit v3 on v2

--- a/solution.py
+++ b/solution.py
@@ -13,7 +13,7 @@
 GRID = 16
 AMPLITUDE = 0.07
 TRUST_FLOOR = 0.02
-RADIUS = 8
+RADIUS = 9
 CHUNKS = 2
 GROUP = 8
 EXTRA = 4
@@ -147,10 +147,16 @@
     pixels = col_ref.shape[0]
     half = pixels // 2
     rt = rt_ref[0]
+    firsts = [
+        jnp.dot(
+            row_ref[...], patch_ref[src_ref[step * GROUP + k]], preferred_element_type=jnp.float32
+        ).astype(jnp.bfloat16)
+        for k in range(GROUP)
+    ]
+    boths = [jnp.dot(f, col_ref[...], preferred_element_type=jnp.float32) for f in firsts]
+    sides = [line_dot(side_ref[...], f[:pixels]) for f in firsts]
     for k in range(GROUP):
-        patch = patch_ref[src_ref[step * GROUP + k]]
-        first = jnp.dot(row_ref[...], patch, preferred_element_type=jnp.float32).astype(jnp.bfloat16)
-        both = jnp.dot(first, col_ref[...], preferred_element_type=jnp.float32)
+        both, side = boths[k], sides[k]
         re = both[:half, :pixels] - both[half:pixels, pixels:]
         im = -(both[:half, pixels:] + both[half:pixels, :pixels])
         cy, sy = rt[:, k : k + 1], rt[:, GROUP + k : GROUP + k + 1]
@@ -162,7 +168,6 @@
         out_re[k] = re * er - im * ei
         out_im[k] = re * ei + im * er
         out_ctf[k] = qc * pc + qs * ps
-        side = line_dot(side_ref[...], first[:pixels])
         low, high = both[pixels : pixels + 1], both[pixels + 1 : pixels + 2]
         edge_ref[0, k : k + 1, :] = low[:, :pixels] - high[:, pixels:]
         edge_ref[1, k : k + 1, :] = -(low[:, pixels:] + high[:, :pixels])
@@ -414,7 +419,7 @@
             sent.append(lax.ppermute(block, ("dom", "rep"), ring(1)))
         ring_blocks.append(sent)
 
-    later = made[0][1][0, 0, 0].astype(jnp.int32)
+    later = made[-1][1][0, 0, 0].astype(jnp.int32)
 
     chosen_view = slot_view[0, :, 0]
     owner_of = chosen_view // view_dev

time: 381 us -> 376 us (0.987)
  Pallas kernels: 69.2 us -> 59.2 us
    ppermute x8 -> x7, waiting for transfers between devices: 24 us -> 9.82 us  [on_device(): arrived[RADIUS + j] = lax.ppermute(sent[j - 1], ('dom', 'rep'), ring(j))]
    ppermute x16 -> x18, waiting for transfers between devices: 53.5 us -> 65.1 us  [on_device(): sent.append(lax.ppermute(block, ('dom', 'rep'), ring(1)))]
    pallas_call x4, Pallas kernels: 31.4 us -> 21.2 us  [spectra(): pl.pallas_call(functools.partial(dft_kernel, start=start), grid=(groups,)...]
    ppermute x8 -> x7, starting transfers between devices: 39.4 us -> 35 us  [on_device(): arrived[RADIUS + j] = lax.ppermute(sent[j - 1], ('dom', 'rep'), ring(j))]
    ppermute x16 -> x18, starting transfers between devices: 34.8 us -> 38.4 us  [on_device(): sent.append(lax.ppermute(block, ('dom', 'rep'), ring(1)))]
  transfers between devices with their start and end apart: 26 -> 27, of which waited for: 14 -> 17; matrix products, arithmetic and copies ran while one was open for 7% -> 8% of each run, Pallas kernels for 15% -> 12%
where the time goes in v3:
time: 376 us; the launch traced here: 373 us
  starting transfers between devices  121 us (32%)
  waiting for transfers between devices  92.8 us (25%)
  Pallas kernels  59.2 us (16%)
  blocking collectives  58 us (15%)
  other arithmetic  22.7 us (6%)
  local copies, waits for them, and re-layouts  16.1 us (4%)
    ppermute x18, waiting for transfers between devices, on_device(): sent.append(lax.ppermute(block, ('dom', 'rep'), ring(1)))  65.1 us
    all_to_all x1, starting transfers between devices, on_device(): heard = lax.all_to_all(asked, 'dom', 0, 0, tiled=True)  45.8 us
    all_gather x1, blocking collectives, on_device(): lax.all_gather(bundle, 'dom', axis=0, axis_index_groups=strides_of)  41.2 us
    ppermute x18, starting transfers between devices, on_device(): sent.append(lax.ppermute(block, ('dom', 'rep'), ring(1)))  38.4 us
    ppermute x7, starting transfers between devices, on_device(): arrived[RADIUS + j] = lax.ppermute(sent[j - 1], ('dom', 'rep'), ring(j))  35 us
    pallas_call x4, Pallas kernels, spectra(): pl.pallas_call(functools.partial(dft_kernel, start=start), grid=(groups,)...  21.2 us
    all_to_all x1, waiting for transfers between devices, on_device(): heard = lax.all_to_all(asked, 'dom', 0, 0, tiled=True)  17.9 us
    pallas_call x4, Pallas kernels, terms_of(): pl.pallas_call(functools.partial(terms_kernel, sources=[(c, f) for _, c,...  17.7 us
  transfers between devices with their start and end apart: 27, of which 17 were waited for; matrix products, arithmetic and copies ran while one was open for 8% of the time, Pallas kernels for 12%

profile of v3, /device:TPU:46, one launch (start us, length us, event | category | flops | bytes accessed | tf_op | source)
XLA Modules:
  0.0 372.9 jit_solution(5874850286159116554)
XLA Ops:
  0.6 2.0 collective-permute-start
  8.4 45.8 %all-to-all-start = ((f32[32,1,18]{2,1,0:T(1,128)}), f32[32,1,18]{2,1,0:T(1,128)S(1)}, u32[]{:S(2)}, u32[]{:S(2)}) async-start(f32[32,1,18]{2,1,0:T(1,128)} %copy.45), calls=%async_computation | async-start | bytes 32768 | tf_op jit(solution)/shard_map/all_to_all | solution.py:469
  57.9 17.9 %all-to-all-done = f32[32,1,18]{2,1,0:T(1,128)S(1)} async-done(((f32[32,1,18]{2,1,0:T(1,128)}), f32[32,1,18]{2,1,0:T(1,128)S(1)}, u32[]{:S(2)}, u32[]{:S(2)}) %all-to-all-start) | async-done | bytes 2336 | tf_op jit(solution)/shard_map/all_to_all | solution.py:469
  77.0 0.9 multiply_cosine_fusion.1
  80.6 1.1 copy-done
  81.7 3.9 %fold.3 = (bf16[2640,128]{1,0:T(8,128)(2,1)}, f32[20,64,128]{2,1,0:T(8,128)}) custom-call(s32[1]{0:T(128)} %bitcast.3.rep_ref, bf16[4,10,2,64,128]{4,3,2,1,0:T(8,128)(2,1)} %own_ref.3, bf16[4,10,2,64,128]{4,3,2,1,0:T(8,128)(2,1)} %copy-done), custom_call_target="tpu_custom_call" | custom-call | tf_op jit(solution)/shard_map/fold/pallas_call | solution.py:124
  85.6 1.2 slice.117
  87.5 3.9 %fold.2 = (bf16[2640,128]{1,0:T(8,128)(2,1)}, f32[20,64,128]{2,1,0:T(8,128)}) custom-call(s32[1]{0:T(128)} %bitcast.3.rep_ref, bf16[4,10,2,64,128]{4,3,2,1,0:T(8,128)(2,1)} %own_ref.3, bf16[4,10,2,64,128]{4,3,2,1,0:T(8,128)(2,1)} %copy-done), custom_call_target="tpu_custom_call" | custom-call | tf_op jit(solution)/shard_map/fold/pallas_call | solution.py:124
  91.4 2.4 collective-permute-start.1
  93.9 2.4 collective-permute-start.2
  96.9 8.7 %collective-permute-done.1.refs_2_ = bf16[2640,128]{1,0:T(8,128)(2,1)S(1)} collective-permute-done((bf16[2640,128]{1,0:T(8,128)(2,1)}, bf16[2640,128]{1,0:T(8,128)(2,1)S(1)}, u32[]{:S(2)}, u32[]{:S(2)}) %collective-permute-start.1) | collective-permute-done | bytes 675872 | tf_op jit(solution)/shard_map/ppermute | solution.py:419
  105.6 1.9 collective-permute-start.3
  107.5 5.3 %collective-permute-done.2.refs_3_ = bf16[2640,128]{1,0:T(8,128)(2,1)S(1)} collective-permute-done((bf16[2640,128]{1,0:T(8,128)(2,1)S(1)}, bf16[2640,128]{1,0:T(8,128)(2,1)S(1)}, u32[]{:S(2)}, u32[]{:S(2)}) %collective-permute-start.2) | collective-permute-done | bytes 675872 | tf_op jit(solution)/shard_map/ppermute | solution.py:419
  112.8 1.9 collective-permute-start.4
  117.0 3.1 collective-permute-done.3.refs_4_
  120.0 1.9 collective-permute-start.5
  122.0 5.3 %collective-permute-done.4.refs_5_ = bf16[2640,128]{1,0:T(8,128)(2,1)S(1)} collective-permute-done((bf16[2640,128]{1,0:T(8,128)(2,1)S(1)}, bf16[2640,128]{1,0:T(8,128)(2,1)S(1)}, u32[]{:S(2)}, u32[]{:S(2)}) %collective-permute-start.4) | collective-permute-done | bytes 675872 | tf_op jit(solution)/shard_map/ppermute | solution.py:419
  127.3 1.9 collective-permute-start.6
  129.2 1.2 slice_bitcast_fusion.2
  134.5 1.9 collective-permute-start.7
  136.5 5.4 %collective-permute-done.6.refs_7_ = bf16[2640,128]{1,0:T(8,128)(2,1)} collective-permute-done((bf16[2640,128]{1,0:T(8,128)(2,1)S(1)}, bf16[2640,128]{1,0:T(8,128)(2,1)}, u32[]{:S(2)}, u32[]{:S(2)}) %collective-permute-start.6) | collective-permute-done | bytes 675872 | tf_op jit(solution)/shard_map/ppermute | solution.py:419
  141.9 1.9 collective-permute-start.8
  143.8 9.1 %apart.1 = f32[112,128]{1,0:T(8,128)} custom-call(s32[112]{0:T(128)} %pad.21.ids_ref, f32[20,64,128]{2,1,0:T(8,128)} %get-tuple-element.55.refs_0_, f32[20,64,128]{2,1,0:T(8,128)} %get-tuple-element.31.refs_1_, f32[14,64,128]{2,1,0:T(8,128)} %pad.23.refs_2_, f32[2,112,128]{2,1,0:T(8,128)} %pad_maximum_fusion.2.refs_3_), custom_call_target="tpu_custom_call" | custom-call | flops 1000000000 | bytes 4000000 | tf_op jit(solution)/shard_map/apart/pallas_call | solution.py:341
  152.9 0.9 reduce_sum.205
  154.9 5.1 %spectra.4 = (f32[24,64,128]{2,1,0:T(8,128)}, f32[24,64,128]{2,1,0:T(8,128)}, f32[24,64,128]{2,1,0:T(8,128)}, f32[4,24,128]{2,1,0:T(8,128)}) custom-call(s32[104]{0:T(128)} %get-tuple-element.122.src_ref, bf16[128,128,128]{2,1,0:T(8,128)(2,1)} %bitcast.104, bf16[144,128]{1,0:T(8,128)(2,1)} %constant.169.clone.row_ref, ...), custom_call_target="tpu_custom_call" | custom-call | flops 3000000000 | bytes 20000000 | tf_op jit(solution)/shard_map/spectra/pallas_call | solution.py:184
  160.0 2.0 collective-permute-start.9
  161.9 2.3 collective-permute-start.10
  165.5 5.1 %spectra.6 = (f32[24,64,128]{2,1,0:T(8,128)}, f32[24,64,128]{2,1,0:T(8,128)}, f32[24,64,128]{2,1,0:T(8,128)}, f32[4,24,128]{2,1,0:T(8,128)}) custom-call(s32[104]{0:T(128)} %get-tuple-element.122.src_ref, bf16[128,128,128]{2,1,0:T(8,128)(2,1)} %bitcast.105, bf16[144,128]{1,0:T(8,128)(2,1)} %constant.169.clone.row_ref, ...), custom_call_target="tpu_custom_call" | custom-call | flops 3000000000 | bytes 20000000 | tf_op jit(solution)/shard_map/spectra/pallas_call | solution.py:184
  170.6 5.1 %spectra.5 = (f32[24,64,128]{2,1,0:T(8,128)}, f32[24,64,128]{2,1,0:T(8,128)}, f32[24,64,128]{2,1,0:T(8,128)}, f32[4,24,128]{2,1,0:T(8,128)}) custom-call(s32[104]{0:T(128)} %get-tuple-element.122.src_ref, bf16[128,128,128]{2,1,0:T(8,128)(2,1)} %bitcast.106, bf16[144,128]{1,0:T(8,128)(2,1)} %constant.169.clone.row_ref, ...), custom_call_target="tpu_custom_call" | custom-call | flops 3000000000 | bytes 20000000 | tf_op jit(solution)/shard_map/spectra/pallas_call | solution.py:184
  175.7 3.6 collective-permute-start.11
  179.3 2.0 collective-permute-done.10.refs_3_
  181.4 1.9 collective-permute-start.12
  184.2 5.9 %spectra.7 = (f32[32,64,128]{2,1,0:T(8,128)}, f32[32,64,128]{2,1,0:T(8,128)}, f32[32,64,128]{2,1,0:T(8,128)}, f32[4,32,128]{2,1,0:T(8,128)}) custom-call(s32[104]{0:T(128)} %get-tuple-element.122.src_ref, bf16[128,128,128]{2,1,0:T(8,128)(2,1)} %bitcast.107, bf16[144,128]{1,0:T(8,128)(2,1)} %constant.169.clone.row_ref, ...), custom_call_target="tpu_custom_call" | custom-call | flops 4000000000 | bytes 20000000 | tf_op jit(solution)/shard_map/spectra/pallas_call | solution.py:184
  191.0 2.0 collective-permute-start.13
  192.9 4.0 %collective-permute-done.12.refs_5_ = bf16[2640,128]{1,0:T(8,128)(2,1)S(1)} collective-permute-done((bf16[2640,128]{1,0:T(8,128)(2,1)S(1)}, bf16[2640,128]{1,0:T(8,128)(2,1)S(1)}, u32[]{:S(2)}, u32[]{:S(2)}) %collective-permute-start.12) | collective-permute-done | bytes 675872 | tf_op jit(solution)/shard_map/ppermute | solution.py:419
  196.9 2.5 collective-permute-start.14
  200.2 4.7 %collective-permute-done.13.refs_6_ = bf16[2640,128]{1,0:T(8,128)(2,1)S(1)} collective-permute-done((bf16[2640,128]{1,0:T(8,128)(2,1)S(1)}, bf16[2640,128]{1,0:T(8,128)(2,1)S(1)}, u32[]{:S(2)}, u32[]{:S(2)}) %collective-permute-start.13) | collective-permute-done | bytes 675872 | tf_op jit(solution)/shard_map/ppermute | solution.py:419
  204.9 1.9 collective-permute-start.15
  206.9 5.3 %collective-permute-done.14.refs_7_ = bf16[2640,128]{1,0:T(8,128)(2,1)S(1)} collective-permute-done((bf16[2640,128]{1,0:T(8,128)(2,1)S(1)}, bf16[2640,128]{1,0:T(8,128)(2,1)S(1)}, u32[]{:S(2)}, u32[]{:S(2)}) %collective-permute-start.14) | collective-permute-done | bytes 675872 | tf_op jit(solution)/shard_map/ppermute | solution.py:419
  212.2 1.9 collective-permute-start.16
  215.0 4.4 %collective-permute-done.15.refs_0_ = bf16[2640,128]{1,0:T(8,128)(2,1)S(1)} collective-permute-done((bf16[2640,128]{1,0:T(8,128)(2,1)S(1)}, bf16[2640,128]{1,0:T(8,128)(2,1)S(1)}, u32[]{:S(2)}, u32[]{:S(2)}) %collective-permute-start.15) | collective-permute-done | bytes 675872 | tf_op jit(solution)/shard_map/ppermute | solution.py:419
  219.4 1.9 collective-permute-start.17
  221.4 5.3 %collective-permute-done.16.refs_1_ = bf16[2640,128]{1,0:T(8,128)(2,1)S(1)} collective-permute-done((bf16[2640,128]{1,0:T(8,128)(2,1)S(1)}, bf16[2640,128]{1,0:T(8,128)(2,1)S(1)}, u32[]{:S(2)}, u32[]{:S(2)}) %collective-permute-start.16) | collective-permute-done | bytes 675872 | tf_op jit(solution)/shard_map/ppermute | solution.py:419
  226.7 1.9 collective-permute-start.18
  229.7 4.2 %collective-permute-done.17.refs_0_.refs_2_ = bf16[2640,128]{1,0:T(8,128)(2,1)S(1)} collective-permute-done((bf16[2640,128]{1,0:T(8,128)(2,1)S(1)}, bf16[2640,128]{1,0:T(8,128)(2,1)S(1)}, u32[]{:S(2)}, u32[]{:S(2)}) %collective-permute-start.17) | collective-permute-done | bytes 675872 | tf_op jit(solution)/shard_map/ppermute | solution.py:419
  233.9 7.2 %collective-permute-done.18.refs_1_.refs_3_ = bf16[2640,128]{1,0:T(8,128)(2,1)S(1)} collective-permute-done((bf16[2640,128]{1,0:T(8,128)(2,1)S(1)}, bf16[2640,128]{1,0:T(8,128)(2,1)S(1)}, u32[]{:S(2)}, u32[]{:S(2)}) %collective-permute-start.18) | collective-permute-done | bytes 675872 | tf_op jit(solution)/shard_map/ppermute | solution.py:419
  242.0 3.4 pick.1
  245.4 1.9 collective-permute-start.19
  247.4 2.1 collective-permute-start.20
  249.5 1.3 broadcast_select_fusion
  250.8 1.5 slice.162.refs_8_
  252.3 2.6 collective-permute-start.21
  254.9 2.7 collective-permute-start.22
  257.6 5.6 %collective-permute-start.23 = (bf16[800,128]{1,0:T(8,128)(2,1)}, bf16[800,128]{1,0:T(8,128)(2,1)S(1)}, u32[]{:S(2)}, u32[]{:S(2)}) collective-permute-start(bf16[800,128]{1,0:T(8,128)(2,1)} %get-tuple-element.49), channel_id=1, source_target_pairs={{0,40},{1,217},{8,48},{9,225},{16,56},{17,233},{24,64},{25,241},{3... | collective-permute-start | bytes 614408 | tf_op jit(solution)/shard_map/ppermute | solution.py:542
  263.2 9.0 %collective-permute-start.24 = (bf16[800,128]{1,0:T(8,128)(2,1)}, bf16[800,128]{1,0:T(8,128)(2,1)S(1)}, u32[]{:S(2)}, u32[]{:S(2)}) collective-permute-start(bf16[800,128]{1,0:T(8,128)(2,1)} %get-tuple-element.50), channel_id=1, source_target_pairs={{0,48},{1,209},{8,56},{9,217},{16,64},{17,225},{24,72},{25,233},{3... | collective-permute-start | bytes 614408 | tf_op jit(solution)/shard_map/ppermute | solution.py:542
  272.2 5.0 %terms.4 = f32[4,24,128]{2,1,0:T(8,128)} custom-call(s32[104]{0:T(128)} %copy-done.34, bf16[2640,128]{1,0:T(8,128)(2,1)} %get-tuple-element.29.refs_0_, bf16[2640,128]{1,0:T(8,128)(2,1)} %get-tuple-element.30.refs_1_, bf16[2640,128]{1,0:T(8,128)(2,1)} %copy-done.6, bf16[2640,128]{1,0:T(8,128)(2,1)} %copy-done.7, bf16[2640,128]{1,0:T(8,128)(2,1)} %copy-done.8, ...), custom_call_target="tpu_custom_call" | custom-call | flops 1000000000 | bytes 10000000 | tf_op jit(solution)/shard_map/terms/pallas_call | solution.py:271
  277.3 11.1 %collective-permute-start.25 = (bf16[400,128]{1,0:T(8,128)(2,1)}, bf16[400,128]{1,0:T(8,128)(2,1)S(1)}, u32[]{:S(2)}, u32[]{:S(2)}) collective-permute-start(bf16[400,128]{1,0:T(8,128)(2,1)} %get-tuple-element.51), channel_id=1, source_target_pairs={{0,56},{1,201},{8,64},{9,209},{16,72},{17,217},{24,80},{25,225},{3... | collective-permute-start | bytes 307208 | tf_op jit(solution)/shard_map/ppermute | solution.py:542
  288.3 5.0 %terms.5 = f32[4,24,128]{2,1,0:T(8,128)} custom-call(s32[104]{0:T(128)} %copy-done.34, bf16[2640,128]{1,0:T(8,128)(2,1)} %collective-permute-done.7.refs_0_, bf16[2640,128]{1,0:T(8,128)(2,1)} %collective-permute-done.8.refs_1_, bf16[2640,128]{1,0:T(8,128)(2,1)} %copy-done.11, bf16[2640,128]{1,0:T(8,128)(2,1)} %copy-done.12, bf16[2640,128]{1,0:T(8,128)(2,1)} %copy-done.13, ...), custom_call_target="tpu_custom_call" | custom-call | flops 1000000000 | bytes 10000000 | tf_op jit(solution)/shard_map/terms/pallas_call | solution.py:271
  293.3 4.1 %terms.6 = f32[4,24,128]{2,1,0:T(8,128)} custom-call(s32[104]{0:T(128)} %copy-done.34, bf16[2640,128]{1,0:T(8,128)(2,1)} %copy-done.3, bf16[2640,128]{1,0:T(8,128)(2,1)} %copy-done.4, bf16[2640,128]{1,0:T(8,128)(2,1)} %copy-done.1, bf16[2640,128]{1,0:T(8,128)(2,1)} %copy-done.2, bf16[800,128]{1,0:T(8,128)(2,1)} %copy-done.22, bf16[800,128]{1,0:T(8,128)(2,1)} %copy-done.23, ...), custom_call_target="tpu_custom_call" | custom-call | flops 1000000000 | bytes 10000000 | tf_op jit(solution)/shard_map/terms/pallas_call | solution.py:271
  297.4 9.0 %collective-permute-done.25.refs_4_ = bf16[400,128]{1,0:T(8,128)(2,1)S(1)} collective-permute-done((bf16[400,128]{1,0:T(8,128)(2,1)}, bf16[400,128]{1,0:T(8,128)(2,1)S(1)}, u32[]{:S(2)}, u32[]{:S(2)}) %collective-permute-start.25) | collective-permute-done | bytes 102432 | tf_op jit(solution)/shard_map/ppermute | solution.py:542
  308.0 3.7 terms.7
  313.2 3.5 all-reduce.5
  316.7 13.4 %all-gather.2 = f32[4,21,256]{2,1,0:T(8,128)S(1)} all-gather(f32[1,21,256]{2,1,0:T(8,128)S(1)} %maximum_bitcast_fusion.2), channel_id=2, replica_groups={{0,8,16,24},{32,40,48,56},{64,72,80,88},{96,104,112,120},{128,136,144,1..., dimensions={0}, use_global_device_ids=true | all-gather | bytes 107520 | tf_op jit(solution)/shard_map/all_gather | solution.py:588
  330.2 41.2 %all-gather.1 = f32[192,256]{1,0:T(8,128)S(1)} all-gather(f32[24,256]{1,0:T(8,128)S(1)} %pad_maximum_fusion.5), channel_id=3, replica_groups={{0,32,64,96,128,160,192,224},{8,40,72,104,136,168,200,232},{16,48,80,11..., dimensions={0}, use_global_device_ids=true | all-gather | bytes 221184 | tf_op jit(solution)/shard_map/all_gather | solution.py:592
  (226 shorter events, 32.1 us)
Async XLA Ops:
  0.6 79.0 %copy-start.48 = (f32[128]{0:T(128)S(1)}, f32[128]{0:T(128)}, u32[]{:S(2)}) copy-start(f32[128]{0:T(128)} %constant.200) | copy-start | bytes 1540
  0.6 80.0 %collective-permute-start = (bf16[4,10,2,64,128]{4,3,2,1,0:T(8,128)(2,1)}, bf16[4,10,2,64,128]{4,3,2,1,0:T(8,128)(2,1)S(1)}, u32[]{:S(2)}, u32[]{:S(2)}) collective-permute-start(bf16[4,10,2,64,128]{4,3,2,1,0:T(8,128)(2,1)} %own_ref.3), channel_id=1, source_target_pairs={{0,1},{1,0},{2,3},{3,2},{4,5},{5,4},{6,7},{7,6},{8,9},{9,8},{10,11... | collective-permute-start | bytes 3932168 | tf_op jit(solution)/shard_map/ppermute | solution.py:400
  8.4 67.5 %all-to-all-start = ((f32[32,1,18]{2,1,0:T(1,128)}), f32[32,1,18]{2,1,0:T(1,128)S(1)}, u32[]{:S(2)}, u32[]{:S(2)}) async-start(f32[32,1,18]{2,1,0:T(1,128)} %copy.45), calls=%async_computation | async-start | bytes 32768 | tf_op jit(solution)/shard_map/all_to_all | solution.py:469
  87.5 6.4 %copy-start.5 = (bf16[2640,128]{1,0:T(8,128)(2,1)S(1)}, bf16[2640,128]{1,0:T(8,128)(2,1)}, u32[]{:S(2)}) copy-start(bf16[2640,128]{1,0:T(8,128)(2,1)} %get-tuple-element.30.refs_1_) | copy-start | bytes 2027524
  87.5 28.3 %copy-start.27 = (f32[10,2,256]{2,1,0:T(2,128)S(1)}, f32[10,2,256]{2,1,0:T(2,128)}, u32[]{:S(2)}) copy-start(f32[10,2,256]{2,1,0:T(2,128)} %param.27) | copy-start | bytes 61444
  87.5 28.6 %copy-start.50 = (f32[64]{0:T(128)S(1)}, f32[64]{0:T(128)}, u32[]{:S(2)}) copy-start(f32[64]{0:T(128)} %constant.198) | copy-start | bytes 772
  91.4 14.1 %collective-permute-start.1 = (bf16[2640,128]{1,0:T(8,128)(2,1)}, bf16[2640,128]{1,0:T(8,128)(2,1)S(1)}, u32[]{:S(2)}, u32[]{:S(2)}) collective-permute-start(bf16[2640,128]{1,0:T(8,128)(2,1)} %get-tuple-element.29.refs_0_), channel_id=1, source_target_pairs={{0,8},{1,249},{8,16},{9,1},{16,24},{17,9},{24,32},{25,17},{32,40},... | collective-permute-start | bytes 2027528 | tf_op jit(solution)/shard_map/ppermute | solution.py:419
  93.9 18.9 %collective-permute-start.2 = (bf16[2640,128]{1,0:T(8,128)(2,1)S(1)}, bf16[2640,128]{1,0:T(8,128)(2,1)S(1)}, u32[]{:S(2)}, u32[]{:S(2)}) collective-permute-start(bf16[2640,128]{1,0:T(8,128)(2,1)S(1)} %copy-done.5), channel_id=1, source_target_pairs={{0,8},{1,249},{8,16},{9,1},{16,24},{17,9},{24,32},{25,17},{32,40},... | collective-permute-start | bytes 2027528 | tf_op jit(solution)/shard_map/ppermute | solution.py:419
  96.8 20.2 %copy-start.31 = (pred[104,10]{0,1:T(8,128)(4,1)}, pred[104,10]{0,1:T(8,128)(4,1)S(1)}, u32[]{:S(2)}) copy-start(pred[104,10]{0,1:T(8,128)(4,1)S(1)} %iota_compare_fusion.6) | copy-start | bytes 3124
  105.6 26.6 %copy-start.6 = (bf16[2640,128]{1,0:T(8,128)(2,1)}, bf16[2640,128]{1,0:T(8,128)(2,1)S(1)}, u32[]{:S(2)}) copy-start(bf16[2640,128]{1,0:T(8,128)(2,1)S(1)} %collective-permute-done.1.refs_2_) | copy-start | bytes 2027524
  105.6 14.5 %collective-permute-start.3 = (bf16[2640,128]{1,0:T(8,128)(2,1)S(1)}, bf16[2640,128]{1,0:T(8,128)(2,1)S(1)}, u32[]{:S(2)}, u32[]{:S(2)}) collective-permute-start(bf16[2640,128]{1,0:T(8,128)(2,1)S(1)} %collective-permute-done.1.refs_2_), channel_id=1, source_target_pairs={{0,8},{1,249},{8,16},{9,1},{16,24},{17,9},{24,32},{25,17},{32,40},... | collective-permute-start | bytes 2027528 | tf_op jit(solution)/shard_map/ppermute | solution.py:419
  112.8 40.1 %copy-start.7 = (bf16[2640,128]{1,0:T(8,128)(2,1)}, bf16[2640,128]{1,0:T(8,128)(2,1)S(1)}, u32[]{:S(2)}) copy-start(bf16[2640,128]{1,0:T(8,128)(2,1)S(1)} %collective-permute-done.2.refs_3_) | copy-start | bytes 2027524
  112.8 14.5 %collective-permute-start.4 = (bf16[2640,128]{1,0:T(8,128)(2,1)S(1)}, bf16[2640,128]{1,0:T(8,128)(2,1)S(1)}, u32[]{:S(2)}, u32[]{:S(2)}) collective-permute-start(bf16[2640,128]{1,0:T(8,128)(2,1)S(1)} %collective-permute-done.2.refs_3_), channel_id=1, source_target_pairs={{0,8},{1,249},{8,16},{9,1},{16,24},{17,9},{24,32},{25,17},{32,40},... | collective-permute-start | bytes 2027528 | tf_op jit(solution)/shard_map/ppermute | solution.py:419
  120.0 32.9 %copy-start.8 = (bf16[2640,128]{1,0:T(8,128)(2,1)}, bf16[2640,128]{1,0:T(8,128)(2,1)S(1)}, u32[]{:S(2)}) copy-start(bf16[2640,128]{1,0:T(8,128)(2,1)S(1)} %collective-permute-done.3.refs_4_) | copy-start | bytes 2027524
  120.0 14.5 %collective-permute-start.5 = (bf16[2640,128]{1,0:T(8,128)(2,1)S(1)}, bf16[2640,128]{1,0:T(8,128)(2,1)S(1)}, u32[]{:S(2)}, u32[]{:S(2)}) collective-permute-start(bf16[2640,128]{1,0:T(8,128)(2,1)S(1)} %collective-permute-done.3.refs_4_), channel_id=1, source_target_pairs={{0,8},{1,249},{8,16},{9,1},{16,24},{17,9},{24,32},{25,17},{32,40},... | collective-permute-start | bytes 2027528 | tf_op jit(solution)/shard_map/ppermute | solution.py:419
  127.3 25.6 %copy-start.9 = (bf16[2640,128]{1,0:T(8,128)(2,1)}, bf16[2640,128]{1,0:T(8,128)(2,1)S(1)}, u32[]{:S(2)}) copy-start(bf16[2640,128]{1,0:T(8,128)(2,1)S(1)} %collective-permute-done.4.refs_5_) | copy-start | bytes 2027524
  127.3 14.6 %collective-permute-start.6 = (bf16[2640,128]{1,0:T(8,128)(2,1)S(1)}, bf16[2640,128]{1,0:T(8,128)(2,1)}, u32[]{:S(2)}, u32[]{:S(2)}) collective-permute-start(bf16[2640,128]{1,0:T(8,128)(2,1)S(1)} %collective-permute-done.4.refs_5_), channel_id=1, source_target_pairs={{0,8},{1,249},{8,16},{9,1},{16,24},{17,9},{24,32},{25,17},{32,40},... | collective-permute-start | bytes 2027528 | tf_op jit(solution)/shard_map/ppermute | solution.py:419
  134.5 18.4 %copy-start.10 = (bf16[2640,128]{1,0:T(8,128)(2,1)}, bf16[2640,128]{1,0:T(8,128)(2,1)S(1)}, u32[]{:S(2)}) copy-start(bf16[2640,128]{1,0:T(8,128)(2,1)S(1)} %collective-permute-done.5.refs_6_) | copy-start | bytes 2027524
  134.5 25.4 %collective-permute-start.7 = (bf16[2640,128]{1,0:T(8,128)(2,1)S(1)}, bf16[2640,128]{1,0:T(8,128)(2,1)}, u32[]{:S(2)}, u32[]{:S(2)}) collective-permute-start(bf16[2640,128]{1,0:T(8,128)(2,1)S(1)} %collective-permute-done.5.refs_6_), channel_id=1, source_target_pairs={{0,8},{1,249},{8,16},{9,1},{16,24},{17,9},{24,32},{25,17},{32,40},... | collective-permute-start | bytes 2027528 | tf_op jit(solution)/shard_map/ppermute | solution.py:419
  141.9 20.1 %collective-permute-start.8 = (bf16[2640,128]{1,0:T(8,128)(2,1)}, bf16[2640,128]{1,0:T(8,128)(2,1)}, u32[]{:S(2)}, u32[]{:S(2)}) collective-permute-start(bf16[2640,128]{1,0:T(8,128)(2,1)} %collective-permute-done.6.refs_7_), channel_id=1, source_target_pairs={{0,8},{1,249},{8,16},{9,1},{16,24},{17,9},{24,32},{25,17},{32,40},... | collective-permute-start | bytes 2027528 | tf_op jit(solution)/shard_map/ppermute | solution.py:419
  143.8 10.0 %copy-start.35 = (f32[104]{0:T(128)S(1)}, f32[104]{0:T(128)}, u32[]{:S(2)}) copy-start(f32[104]{0:T(128)} %get-tuple-element.107) | copy-start | bytes 1252
  143.8 10.0 %copy-start.53 = (f32[128]{0:T(128)S(1)}, f32[128]{0:T(128)}, u32[]{:S(2)}) copy-start(f32[128]{0:T(128)} %constant.199) | copy-start | bytes 1540
  160.0 15.8 %collective-permute-start.9 = (bf16[2640,128]{1,0:T(8,128)(2,1)}, bf16[2640,128]{1,0:T(8,128)(2,1)S(1)}, u32[]{:S(2)}, u32[]{:S(2)}) collective-permute-start(bf16[2640,128]{1,0:T(8,128)(2,1)} %collective-permute-done.7.refs_0_), channel_id=1, source_target_pairs={{0,8},{1,249},{8,16},{9,1},{16,24},{17,9},{24,32},{25,17},{32,40},... | collective-permute-start | bytes 2027528 | tf_op jit(solution)/shard_map/ppermute | solution.py:419
  161.9 19.4 %collective-permute-start.10 = (bf16[2640,128]{1,0:T(8,128)(2,1)}, bf16[2640,128]{1,0:T(8,128)(2,1)S(1)}, u32[]{:S(2)}, u32[]{:S(2)}) collective-permute-start(bf16[2640,128]{1,0:T(8,128)(2,1)} %collective-permute-done.8.refs_1_), channel_id=1, source_target_pairs={{0,8},{1,249},{8,16},{9,1},{16,24},{17,9},{24,32},{25,17},{32,40},... | collective-permute-start | bytes 2027528 | tf_op jit(solution)/shard_map/ppermute | solution.py:419
  170.6 13.5 %copy-start.30 = (f32[4,24,128]{2,1,0:T(8,128)S(1)}, f32[4,24,128]{2,1,0:T(8,128)}, u32[]{:S(2)}) copy-start(f32[4,24,128]{2,1,0:T(8,128)} %get-tuple-element.37) | copy-start | bytes 147460
  175.7 14.3 %copy-start.11 = (bf16[2640,128]{1,0:T(8,128)(2,1)}, bf16[2640,128]{1,0:T(8,128)(2,1)S(1)}, u32[]{:S(2)}) copy-start(bf16[2640,128]{1,0:T(8,128)(2,1)S(1)} %collective-permute-done.9.refs_2_) | copy-start | bytes 2027524
  175.7 15.2 %collective-permute-start.11 = (bf16[2640,128]{1,0:T(8,128)(2,1)S(1)}, bf16[2640,128]{1,0:T(8,128)(2,1)S(1)}, u32[]{:S(2)}, u32[]{:S(2)}) collective-permute-start(bf16[2640,128]{1,0:T(8,128)(2,1)S(1)} %collective-permute-done.9.refs_2_), channel_id=1, source_target_pairs={{0,8},{1,249},{8,16},{9,1},{16,24},{17,9},{24,32},{25,17},{32,40},... | collective-permute-start | bytes 2027528 | tf_op jit(solution)/shard_map/ppermute | solution.py:419
  181.4 8.7 %copy-start.12 = (bf16[2640,128]{1,0:T(8,128)(2,1)}, bf16[2640,128]{1,0:T(8,128)(2,1)S(1)}, u32[]{:S(2)}) copy-start(bf16[2640,128]{1,0:T(8,128)(2,1)S(1)} %collective-permute-done.10.refs_3_) | copy-start | bytes 2027524
  181.4 15.6 %collective-permute-start.12 = (bf16[2640,128]{1,0:T(8,128)(2,1)S(1)}, bf16[2640,128]{1,0:T(8,128)(2,1)S(1)}, u32[]{:S(2)}, u32[]{:S(2)}) collective-permute-start(bf16[2640,128]{1,0:T(8,128)(2,1)S(1)} %collective-permute-done.10.refs_3_), channel_id=1, source_target_pairs={{0,8},{1,249},{8,16},{9,1},{16,24},{17,9},{24,32},{25,17},{32,40},... | collective-permute-start | bytes 2027528 | tf_op jit(solution)/shard_map/ppermute | solution.py:419
  184.1 15.3 %copy-start.36 = (f32[128]{0:T(128)S(1)}, f32[128]{0:T(128)}, u32[]{:S(2)}) copy-start(f32[128]{0:T(128)} %constant.201) | copy-start | bytes 1540
  184.1 15.3 %copy-start.40 = (f32[104]{0:T(128)S(1)}, f32[104]{0:T(128)}, u32[]{:S(2)}) copy-start(f32[104]{0:T(128)} %get-tuple-element.105) | copy-start | bytes 1252
  184.1 30.0 %copy-start.41 = (f32[104]{0:T(128)S(1)}, f32[104]{0:T(128)}, u32[]{:S(2)}) copy-start(f32[104]{0:T(128)} %get-tuple-element.113) | copy-start | bytes 1252
  184.2 30.0 %copy-start.52 = (f32[128]{0:T(128)S(1)}, f32[128]{0:T(128)}, u32[]{:S(2)}) copy-start(f32[128]{0:T(128)} %constant.202) | copy-start | bytes 1540
  184.2 30.3 %copy-start.38 = (f32[104]{0:T(128)S(1)}, f32[104]{0:T(128)}, u32[]{:S(2)}) copy-start(f32[104]{0:T(128)} %get-tuple-element.104) | copy-start | bytes 1252
  184.2 30.3 %copy-start.39 = (f32[104]{0:T(128)S(1)}, f32[104]{0:T(128)}, u32[]{:S(2)}) copy-start(f32[104]{0:T(128)} %get-tuple-element.106) | copy-start | bytes 1252
  184.2 30.3 %copy-start.47 = (f32[128]{0:T(128)S(1)}, f32[128]{0:T(128)}, u32[]{:S(2)}) copy-start(f32[128]{0:T(128)} %constant.203) | copy-start | bytes 1540
  190.1 38.5 %copy-start.32 = (pred[104,10]{0,1:T(8,128)(4,1)S(1)}, pred[104,10]{0,1:T(8,128)(4,1)}, u32[]{:S(2)}) copy-start(pred[104,10]{0,1:T(8,128)(4,1)} %copy-done.31) | copy-start | bytes 3124
  190.1 38.5 %copy-start.42 = (f32[104]{0:T(128)S(1)}, f32[104]{0:T(128)}, u32[]{:S(2)}) copy-start(f32[104]{0:T(128)} %get-tuple-element.113) | copy-start | bytes 1252
  190.1 38.5 %copy-start.51 = (f32[128]{0:T(128)S(1)}, f32[128]{0:T(128)}, u32[]{:S(2)}) copy-start(f32[128]{0:T(128)} %constant.204) | copy-start | bytes 1540
  191.0 9.2 %copy-start.13 = (bf16[2640,128]{1,0:T(8,128)(2,1)}, bf16[2640,128]{1,0:T(8,128)(2,1)S(1)}, u32[]{:S(2)}) copy-start(bf16[2640,128]{1,0:T(8,128)(2,1)S(1)} %collective-permute-done.11.refs_4_) | copy-start | bytes 2027524
  191.0 13.9 %collective-permute-start.13 = (bf16[2640,128]{1,0:T(8,128)(2,1)S(1)}, bf16[2640,128]{1,0:T(8,128)(2,1)S(1)}, u32[]{:S(2)}, u32[]{:S(2)}) collective-permute-start(bf16[2640,128]{1,0:T(8,128)(2,1)S(1)} %collective-permute-done.11.refs_4_), channel_id=1, source_target_pairs={{0,8},{1,249},{8,16},{9,1},{16,24},{17,9},{24,32},{25,17},{32,40},... | collective-permute-start | bytes 2027528 | tf_op jit(solution)/shard_map/ppermute | solution.py:419
  196.9 10.0 %copy-start.14 = (bf16[2640,128]{1,0:T(8,128)(2,1)}, bf16[2640,128]{1,0:T(8,128)(2,1)S(1)}, u32[]{:S(2)}) copy-start(bf16[2640,128]{1,0:T(8,128)(2,1)S(1)} %collective-permute-done.12.refs_5_) | copy-start | bytes 2027524
  196.9 15.2 %collective-permute-start.14 = (bf16[2640,128]{1,0:T(8,128)(2,1)S(1)}, bf16[2640,128]{1,0:T(8,128)(2,1)S(1)}, u32[]{:S(2)}, u32[]{:S(2)}) collective-permute-start(bf16[2640,128]{1,0:T(8,128)(2,1)S(1)} %collective-permute-done.12.refs_5_), channel_id=1, source_target_pairs={{0,8},{1,249},{8,16},{9,1},{16,24},{17,9},{24,32},{25,17},{32,40},... | collective-permute-start | bytes 2027528 | tf_op jit(solution)/shard_map/ppermute | solution.py:419
  204.9 72.3 %copy-start.15 = (bf16[2640,128]{1,0:T(8,128)(2,1)}, bf16[2640,128]{1,0:T(8,128)(2,1)S(1)}, u32[]{:S(2)}) copy-start(bf16[2640,128]{1,0:T(8,128)(2,1)S(1)} %collective-permute-done.13.refs_6_) | copy-start | bytes 2027524
  204.9 14.5 %collective-permute-start.15 = (bf16[2640,128]{1,0:T(8,128)(2,1)S(1)}, bf16[2640,128]{1,0:T(8,128)(2,1)S(1)}, u32[]{:S(2)}, u32[]{:S(2)}) collective-permute-start(bf16[2640,128]{1,0:T(8,128)(2,1)S(1)} %collective-permute-done.13.refs_6_), channel_id=1, source_target_pairs={{0,8},{1,249},{8,16},{9,1},{16,24},{17,9},{24,32},{25,17},{32,40},... | collective-permute-start | bytes 2027528 | tf_op jit(solution)/shard_map/ppermute | solution.py:419
  212.2 9.2 %copy-start.16 = (bf16[2640,128]{1,0:T(8,128)(2,1)}, bf16[2640,128]{1,0:T(8,128)(2,1)S(1)}, u32[]{:S(2)}) copy-start(bf16[2640,128]{1,0:T(8,128)(2,1)S(1)} %collective-permute-done.14.refs_7_) | copy-start | bytes 2027524
  212.2 14.5 %collective-permute-start.16 = (bf16[2640,128]{1,0:T(8,128)(2,1)S(1)}, bf16[2640,128]{1,0:T(8,128)(2,1)S(1)}, u32[]{:S(2)}, u32[]{:S(2)}) collective-permute-start(bf16[2640,128]{1,0:T(8,128)(2,1)S(1)} %collective-permute-done.14.refs_7_), channel_id=1, source_target_pairs={{0,8},{1,249},{8,16},{9,1},{16,24},{17,9},{24,32},{25,17},{32,40},... | collective-permute-start | bytes 2027528 | tf_op jit(solution)/shard_map/ppermute | solution.py:419
  219.4 57.8 %copy-start.3 = (bf16[2640,128]{1,0:T(8,128)(2,1)}, bf16[2640,128]{1,0:T(8,128)(2,1)S(1)}, u32[]{:S(2)}) copy-start(bf16[2640,128]{1,0:T(8,128)(2,1)S(1)} %collective-permute-done.15.refs_0_) | copy-start | bytes 2027524
  219.4 14.5 %collective-permute-start.17 = (bf16[2640,128]{1,0:T(8,128)(2,1)S(1)}, bf16[2640,128]{1,0:T(8,128)(2,1)S(1)}, u32[]{:S(2)}, u32[]{:S(2)}) collective-permute-start(bf16[2640,128]{1,0:T(8,128)(2,1)S(1)} %collective-permute-done.15.refs_0_), channel_id=1, source_target_pairs={{0,8},{1,249},{8,16},{9,1},{16,24},{17,9},{24,32},{25,17},{32,40},... | collective-permute-start | bytes 2027528 | tf_op jit(solution)/shard_map/ppermute | solution.py:419
  226.7 50.6 %copy-start.4 = (bf16[2640,128]{1,0:T(8,128)(2,1)}, bf16[2640,128]{1,0:T(8,128)(2,1)S(1)}, u32[]{:S(2)}) copy-start(bf16[2640,128]{1,0:T(8,128)(2,1)S(1)} %collective-permute-done.16.refs_1_) | copy-start | bytes 2027524
  226.7 14.5 %collective-permute-start.18 = (bf16[2640,128]{1,0:T(8,128)(2,1)S(1)}, bf16[2640,128]{1,0:T(8,128)(2,1)S(1)}, u32[]{:S(2)}, u32[]{:S(2)}) collective-permute-start(bf16[2640,128]{1,0:T(8,128)(2,1)S(1)} %collective-permute-done.16.refs_1_), channel_id=1, source_target_pairs={{0,8},{1,249},{8,16},{9,1},{16,24},{17,9},{24,32},{25,17},{32,40},... | collective-permute-start | bytes 2027528 | tf_op jit(solution)/shard_map/ppermute | solution.py:419
  233.9 7.2 %copy-start.1 = (bf16[2640,128]{1,0:T(8,128)(2,1)}, bf16[2640,128]{1,0:T(8,128)(2,1)S(1)}, u32[]{:S(2)}) copy-start(bf16[2640,128]{1,0:T(8,128)(2,1)S(1)} %collective-permute-done.17.refs_0_.refs_2_) | copy-start | bytes 2027524
  245.4 17.7 %collective-permute-start.19 = (bf16[800,128]{1,0:T(8,128)(2,1)}, bf16[800,128]{1,0:T(8,128)(2,1)S(1)}, u32[]{:S(2)}, u32[]{:S(2)}) collective-permute-start(bf16[800,128]{1,0:T(8,128)(2,1)} %get-tuple-element.42), channel_id=1, source_target_pairs={{0,8},{1,249},{8,16},{9,1},{16,24},{17,9},{24,32},{25,17},{32,40},... | collective-permute-start | bytes 614408 | tf_op jit(solution)/shard_map/ppermute | solution.py:542
  247.4 29.9 %collective-permute-start.20 = (bf16[800,128]{1,0:T(8,128)(2,1)}, bf16[800,128]{1,0:T(8,128)(2,1)S(1)}, u32[]{:S(2)}, u32[]{:S(2)}) collective-permute-start(bf16[800,128]{1,0:T(8,128)(2,1)} %get-tuple-element.43), channel_id=1, source_target_pairs={{0,16},{1,241},{8,24},{9,249},{16,32},{17,1},{24,40},{25,9},{32,48... | collective-permute-start | bytes 614408 | tf_op jit(solution)/shard_map/ppermute | solution.py:542
  252.3 54.1 %collective-permute-start.21 = (bf16[800,128]{1,0:T(8,128)(2,1)}, bf16[800,128]{1,0:T(8,128)(2,1)S(1)}, u32[]{:S(2)}, u32[]{:S(2)}) collective-permute-start(bf16[800,128]{1,0:T(8,128)(2,1)} %get-tuple-element.47), channel_id=1, source_target_pairs={{0,24},{1,233},{8,32},{9,241},{16,40},{17,249},{24,48},{25,1},{32,... | collective-permute-start | bytes 614408 | tf_op jit(solution)/shard_map/ppermute | solution.py:542
  254.9 51.5 %collective-permute-start.22 = (bf16[800,128]{1,0:T(8,128)(2,1)}, bf16[800,128]{1,0:T(8,128)(2,1)S(1)}, u32[]{:S(2)}, u32[]{:S(2)}) collective-permute-start(bf16[800,128]{1,0:T(8,128)(2,1)} %get-tuple-element.48), channel_id=1, source_target_pairs={{0,32},{1,225},{8,40},{9,233},{16,48},{17,241},{24,56},{25,249},{3... | collective-permute-start | bytes 614408 | tf_op jit(solution)/shard_map/ppermute | solution.py:542
  257.6 48.9 %collective-permute-start.23 = (bf16[800,128]{1,0:T(8,128)(2,1)}, bf16[800,128]{1,0:T(8,128)(2,1)S(1)}, u32[]{:S(2)}, u32[]{:S(2)}) collective-permute-start(bf16[800,128]{1,0:T(8,128)(2,1)} %get-tuple-element.49), channel_id=1, source_target_pairs={{0,40},{1,217},{8,48},{9,225},{16,56},{17,233},{24,64},{25,241},{3... | collective-permute-start | bytes 614408 | tf_op jit(solution)/shard_map/ppermute | solution.py:542
  263.1 14.1 %copy-start.22 = (bf16[800,128]{1,0:T(8,128)(2,1)}, bf16[800,128]{1,0:T(8,128)(2,1)S(1)}, u32[]{:S(2)}) copy-start(bf16[800,128]{1,0:T(8,128)(2,1)S(1)} %collective-permute-done.19.refs_4_) | copy-start | bytes 614404
  263.2 44.1 %collective-permute-start.24 = (bf16[800,128]{1,0:T(8,128)(2,1)}, bf16[800,128]{1,0:T(8,128)(2,1)S(1)}, u32[]{:S(2)}, u32[]{:S(2)}) collective-permute-start(bf16[800,128]{1,0:T(8,128)(2,1)} %get-tuple-element.50), channel_id=1, source_target_pairs={{0,48},{1,209},{8,56},{9,217},{16,64},{17,225},{24,72},{25,233},{3... | collective-permute-start | bytes 614408 | tf_op jit(solution)/shard_map/ppermute | solution.py:542
  277.3 16.1 %copy-start.23 = (bf16[800,128]{1,0:T(8,128)(2,1)}, bf16[800,128]{1,0:T(8,128)(2,1)S(1)}, u32[]{:S(2)}) copy-start(bf16[800,128]{1,0:T(8,128)(2,1)S(1)} %collective-permute-done.20.refs_5_) | copy-start | bytes 614404
  277.3 29.1 %collective-permute-start.25 = (bf16[400,128]{1,0:T(8,128)(2,1)}, bf16[400,128]{1,0:T(8,128)(2,1)S(1)}, u32[]{:S(2)}, u32[]{:S(2)}) collective-permute-start(bf16[400,128]{1,0:T(8,128)(2,1)} %get-tuple-element.51), channel_id=1, source_target_pairs={{0,56},{1,201},{8,64},{9,209},{16,72},{17,217},{24,80},{25,225},{3... | collective-permute-start | bytes 307208 | tf_op jit(solution)/shard_map/ppermute | solution.py:542
  311.6 60.4 %copy-start.33 = (s32[8,4]{1,0:T(8,128)S(1)}, s32[8,4]{1,0:T(8,128)}, u32[]{:S(2)}) copy-start(s32[8,4]{1,0:T(8,128)} %multiply_add_fusion) | copy-start | bytes 388
  311.6 60.3 %copy-start.46 = (s32[256]{0:T(256)S(1)}, s32[256]{0:T(256)}, u32[]{:S(2)}) copy-start(s32[256]{0:T(256)} %and_select_fusion) | copy-start | bytes 3076
  311.7 60.4 %copy-start.54 = (pred[128,2]{0,1:T(4,128)(4,1)S(1)}, pred[128,2]{0,1:T(4,128)(4,1)}, u32[]{:S(2)}) copy-start(pred[128,2]{0,1:T(4,128)(4,1)} %iota_compare_fusion.7) | copy-start | bytes 772
  (19 other events, 46.7 us)
